TPU v7x, 768 devices: a whole 4x8x12 slice. The times are simulated.
768 devices in a mesh: dp: 12 (over z), expert: 64 (over y, x, core).
Axes of the slice: x: 4, y: 8, z: 12, core: 2. Of those that a mesh axis runs over, the one named last changes fastest.
Arguments:
- tokens: bfloat16 [2048, 4096], P('expert'), may hold values from -6 to 6
- expert_ids: int32 [2048, 8], P('expert'), may hold values from 0 to 63, all different within a row; in each aligned block of 32 rows (0 to 31, 32 to 63, ...) at most 6 rows name the same one
- gate_ints: int32 [2048, 8], P('expert'), may hold values from 1 to 1024
- w_gate: bfloat16 [64, 4096, 1536], P('expert', None, 'dp'), may hold values from -0.09375 to 0.09375
- w_up: bfloat16 [64, 4096, 1536], P('expert', None, 'dp'), may hold values from -0.09375 to 0.09375
- w_down: bfloat16 [64, 1536, 4096], P('expert', 'dp'), may hold values from -0.15625 to 0.15625
Outputs:
- mixed: bfloat16 [2048, 4096], P('expert')
Inputs may be any that keep to these rules, and one draw needn't show every extreme that they name: `expert_ids`: within the rows of one device each expert is named at most 6 times, and each row names 8 different experts.
All inputs are finite; a program needn't handle non-finite values.
Results may differ from a plain program's by a relative error of at most 0.017.
Values may be sent and summed in bfloat16 or wider, within the bound.
No kernel may reach another device: no remote copies, remote signals or barrier semaphores. Data moves between devices by JAX's collectives and lax.ppermute only.
A program may use at most 64 MiB of HBM per device.

v0:
```python
import jax
import jax.numpy as jnp
from jax import lax
from jax.sharding import PartitionSpec as P


def total_of_pieces(value, axis):
    tiles = lax.all_gather(value, axis).astype(jnp.float32)
    return tiles.sum(axis=0)


def on_device(tokens, expert_ids, gate_ints, w_gate, w_up, w_down):
    tok_rows = tokens.shape[0]
    top_count = expert_ids.shape[1]
    feature = tokens.shape[1]
    groups = lax.axis_size("expert")
    capacity = min(tok_rows, max(2, 3 * tok_rows * top_count // (2 * groups)))
    pairs = tok_rows * top_count
    flat_ids = expert_ids.reshape(pairs)
    onehot = (flat_ids[:, None] == jnp.arange(groups, dtype=jnp.int32)[None, :]).astype(jnp.int32)
    before = jnp.cumsum(onehot, axis=0) - onehot
    slot = jnp.sum(before * onehot, axis=1)
    target = flat_ids * capacity + slot
    select = (jnp.arange(groups * capacity, dtype=jnp.int32)[:, None] == target[None, :]).astype(
        jnp.bfloat16
    )
    owner = (
        (jnp.arange(pairs, dtype=jnp.int32) // top_count)[:, None]
        == jnp.arange(tok_rows, dtype=jnp.int32)[None, :]
    ).astype(jnp.bfloat16)
    placing = jnp.dot(select, owner, preferred_element_type=jnp.float32).astype(jnp.bfloat16)
    outgoing = jnp.dot(placing, tokens, preferred_element_type=jnp.float32).astype(jnp.bfloat16)
    arrived = lax.all_to_all(
        outgoing.reshape(groups, capacity, feature),
        "expert",
        split_axis=0,
        concat_axis=0,
        tiled=True,
    )
    rows = arrived.reshape(groups * capacity, feature)
    gate = jnp.dot(rows, w_gate[0], preferred_element_type=jnp.float32)
    up = jnp.dot(rows, w_up[0], preferred_element_type=jnp.float32)
    hidden = (jax.nn.silu(gate) * up).astype(jnp.bfloat16)
    partial_value = jnp.dot(hidden, w_down[0], preferred_element_type=jnp.float32).astype(
        jnp.bfloat16
    )
    back = lax.all_to_all(
        partial_value.reshape(groups, capacity, feature),
        "expert",
        split_axis=0,
        concat_axis=0,
        tiled=True,
    )
    back_rows = back.reshape(groups * capacity, feature)
    weights = (gate_ints.astype(jnp.float32) / 1024.0)[:, :, None]
    picked = (
        jnp.take(back_rows, target, axis=0)
        .reshape(tok_rows, top_count, feature)
        .astype(jnp.float32)
    )
    local_mix = jnp.sum(weights * picked, axis=1)
    mixed = total_of_pieces(local_mix.astype(jnp.bfloat16), "dp").astype(jnp.float32)
    return mixed.astype(jnp.bfloat16)


def solution(mesh):
    return jax.shard_map(
        on_device,
        mesh=mesh,
        in_specs=(
            P("expert", None),
            P("expert", None),
            P("expert", None),
            P("expert", None, "dp"),
            P("expert", None, "dp"),
            P("expert", "dp", None),
        ),
        out_specs=P("expert", None),
        check_vma=False,
    )
```

profile of v0, /device:TPU:2, one launch (start us, length us, event | category | flops | bytes accessed | tf_op | source)
XLA Modules:
  0.0 338.9 jit_solution(9721100982008217303)
XLA Ops:
  6.5 0.8 copy.15
  7.4 0.1 eq.52
  7.5 0.1 reshape.104
  7.6 0.6 reduce-window.6
  8.2 0.2 slice_reduce_fusion
  8.4 0.1 fusion.16
  8.5 3.9 %convolution_convert_fusion = bf16[384,4096]{1,0:T(8,128)(2,1)} fusion(bf16[32,4096]{1,0:T(8,128)(2,1)} %param.6, s32[256]{0:T(256)S(1)} %get-tuple-element.6, s32[256]{0:T(256)S(1)} %get-tuple-element.5), kind=kOutput, calls=%fused_computation.1 | convolution fusion | flops 108646400 | bytes 3409920 | tf_op jit(solution)/shard_map/dot_general | solution.py:32
  12.4 5.6 %reshape.106 = bf16[64,6,4096]{2,1,0:T(8,128)(2,1)} reshape(bf16[384,4096]{1,0:T(8,128)(2,1)} %convolution_convert_fusion) | data formatting | bytes 6291456 | tf_op jit(solution)/shard_map/reshape | solution.py:34
  18.1 110.8 %all_to_all.10 = bf16[64,6,4096]{2,1,0:T(8,128)(2,1)} all-to-all(bf16[64,6,4096]{2,1,0:T(8,128)(2,1)} %reshape.106), channel_id=1, replica_groups=mesh['dp'=12,'expert'=64] {'expert'}, dimensions={0} | all-to-all | bytes 6291456 | tf_op jit(solution)/shard_map/all_to_all | solution.py:33
  128.9 5.8 %reshape.107 = bf16[384,4096]{1,0:T(8,128)(2,1)} reshape(bf16[64,6,4096]{2,1,0:T(8,128)(2,1)} %all_to_all.10) | data formatting | bytes 6291456 | tf_op jit(solution)/shard_map/reshape | solution.py:40
  134.7 2.9 fusion.4
  137.7 7.1 %convolution_convert_fusion.1 = bf16[384,4096]{1,0:T(8,128)(2,1)} fusion(bf16[384,4096]{1,0:T(8,128)(2,1)} %reshape.107, bf16[1,128,4096]{2,1,0:T(8,128)(2,1)S(1)} %copy-done, bf16[1,4096,128]{2,1,0:T(8,128)(2,1)S(1)} %copy-done.2, f32[384,128]{1,0:T(8,128)S(1)} %fusion.4), kind=kOutput, calls=%fused_computation.2 | convolution fusion | flops 807174144 | bytes 8585216 | tf_op jit(solution)/shard_map/dot_general | solution.py:44
  144.8 5.6 %reshape.108 = bf16[64,6,4096]{2,1,0:T(8,128)(2,1)} reshape(bf16[384,4096]{1,0:T(8,128)(2,1)} %convolution_convert_fusion.1) | data formatting | bytes 6291456 | tf_op jit(solution)/shard_map/reshape | solution.py:48
  150.4 5.8 %all-to-all-start.1 = ((bf16[64,6,4096]{2,1,0:T(8,128)(2,1)}), bf16[64,6,4096]{2,1,0:T(8,128)(2,1)}, u32[]{:S(2)}, u32[]{:S(2)}) async-start(bf16[64,6,4096]{2,1,0:T(8,128)(2,1)} %reshape.108), calls=%async_computation.1 | async-start | bytes 8388608 | tf_op jit(solution)/shard_map/all_to_all | solution.py:47
  156.2 0.2 all-gather.3.cloned.1.call-start
  156.4 0.1 reduce_sum.35
  156.5 0.1 mul.53
  156.6 0.1 copy.14
  156.7 95.6 %all-to-all-done.1 = bf16[64,6,4096]{2,1,0:T(8,128)(2,1)} async-done(((bf16[64,6,4096]{2,1,0:T(8,128)(2,1)}), bf16[64,6,4096]{2,1,0:T(8,128)(2,1)}, u32[]{:S(2)}, u32[]{:S(2)}) %all-to-all-start.1) | async-done | bytes 3145760 | tf_op jit(solution)/shard_map/all_to_all | solution.py:47
  252.4 5.7 %reshape.109 = bf16[384,4096]{1,0:T(8,128)(2,1)} reshape(bf16[64,6,4096]{2,1,0:T(8,128)(2,1)} %all-to-all-done.1) | data formatting | bytes 6291456 | tf_op jit(solution)/shard_map/reshape | solution.py:54
  258.1 6.2 %gather_fusion = bf16[256,4096]{1,0:T(8,128)(2,1)S(1)} fusion(bf16[384,4096]{1,0:T(8,128)(2,1)} %reshape.109, s32[1024]{0:T(1024)S(1)} %pad_clamp_fusion), kind=kCustom, calls=%fused_computation | custom fusion | bytes 4195328 | tf_op jit(solution)/shard_map/jit(_take)/gather | solution.py:57
  264.3 2.6 multiply_reduce_fusion
  266.9 61.9 %all-gather.3.cloned.1.call-done = bf16[384,4096]{1,0:T(8,128)(2,1)} async-done(((bf16[32,4096]{1,0:T(8,128)(2,1)}), bf16[384,4096]{1,0:T(8,128)(2,1)}) %all-gather.3.cloned.1.call-update) | async-done | bytes 3145744 | tf_op jit(solution)/shard_map/all_gather | solution.py:8
  328.8 3.2 reduce_sum.38
  (18 shorter events, 0.1 us)
Async XLA Ops:
  6.5 131.2 %copy-start = (bf16[1,128,4096]{2,1,0:T(8,128)(2,1)S(1)}, bf16[1,128,4096]{2,1,0:T(8,128)(2,1)}, u32[]{:S(2)}) copy-start(bf16[1,128,4096]{2,1,0:T(8,128)(2,1)} %param.11) | copy-start | bytes 3145732
  128.9 5.8 %copy-start.1 = (bf16[1,4096,128]{2,1,0:T(8,128)(2,1)S(1)}, bf16[1,4096,128]{2,1,0:T(8,128)(2,1)}, u32[]{:S(2)}) copy-start(bf16[1,4096,128]{2,1,0:T(8,128)(2,1)} %param.9) | copy-start | bytes 3145732
  134.7 3.0 copy-start.2
  150.4 6.2 %copy-start.3 = (s32[32,8]{0,1:T(8,128)S(1)}, s32[32,8]{0,1:T(8,128)}, u32[]{:S(2)}) copy-start(s32[32,8]{0,1:T(8,128)} %param.8) | copy-start | bytes 3076
  150.4 101.9 %all-to-all-start.1 = ((bf16[64,6,4096]{2,1,0:T(8,128)(2,1)}), bf16[64,6,4096]{2,1,0:T(8,128)(2,1)}, u32[]{:S(2)}, u32[]{:S(2)}) async-start(bf16[64,6,4096]{2,1,0:T(8,128)(2,1)} %reshape.108), calls=%async_computation.1 | async-start | bytes 8388608 | tf_op jit(solution)/shard_map/all_to_all | solution.py:47
  156.2 172.6 %all-gather.3.cloned.1.call-start = ((), (), s32[]{:S(2)}) async-start(), calls=%async_computation.2 | async-start | bytes 3407872 | tf_op jit(solution)/shard_map/all_gather | solution.py:8
Sparse Core Ops, SparseCore 0:
  267.0 61.7 all-gather.2
where the time goes:
time: 340 us; the launch traced here: 339 us
  waiting for transfers between devices  158 us (46%)
  blocking collectives  111 us (33%)
  local copies, waits for them, and re-layouts  30.5 us (9%)
  matrix products  13.9 us (4%)
  between operations  13.5 us (4%)
  other arithmetic  6.61 us (2%)
  starting transfers between devices  5.97 us (2%)
    all_to_all x1, blocking collectives, on_device(): lax.all_to_all(outgoing.reshape(groups, capacity, feature), 'expert', spl...  111 us
    all_to_all x1, waiting for transfers between devices, on_device(): lax.all_to_all(partial_value.reshape(groups, capacity, feature), 'expert'...  95.6 us
    all_gather x1, waiting for transfers between devices, total_of_pieces(): tiles = lax.all_gather(value, axis).astype(jnp.float32)  61.9 us
    dot_general x1, matrix products, on_device(): jnp.dot(hidden, w_down[0], preferred_element_type=jnp.float32)  7.07 us
  transfers between devices with their start and end apart: 2, of which 2 were waited for; matrix products, arithmetic and copies ran while one was open for 0% of the time, Pallas kernels for 0%

commit v1 on v0

v1 whole, which is shorter than its diff:
```python
import jax
import jax.numpy as jnp
from jax import lax
from jax.sharding import PartitionSpec as P

BF16 = jnp.bfloat16
F32 = jnp.float32


def partner_pairs(n_dp, n_expert, step):
    pairs = []
    for p in range(n_dp):
        for e in range(n_expert):
            shift = e % 2
            other = ((((p - shift) % n_dp) ^ step) + shift) % n_dp
            pairs.append((p * n_expert + e, other * n_expert + e))
    return pairs


def exchange(x, pairs):
    return lax.ppermute(x, ("dp", "expert"), pairs)


def on_device(tokens, expert_ids, gate_ints, w_gate, w_up, w_down):
    n_dp, groups = lax.axis_size("dp"), lax.axis_size("expert")
    tok_rows, feature = tokens.shape
    top = expert_ids.shape[1]
    cap = min(tok_rows, max(2, 3 * tok_rows * top // (2 * groups)))
    rows = groups * cap
    half, quarter = feature // 2, feature // 4
    ff = w_gate.shape[2]
    p = lax.axis_index("dp")
    a, b = p % 2, (p // 2) % 2
    near = partner_pairs(n_dp, groups, 1)
    far = partner_pairs(n_dp, groups, 2)

    wg, wu, wd = w_gate[0], w_up[0], w_down[0]
    got_g = exchange(lax.dynamic_slice(wg, ((1 - a) * half, 0), (half, ff)), near)
    got_u = exchange(lax.dynamic_slice(wu, ((1 - a) * half, 0), (half, ff)), near)
    got_d = exchange(lax.dynamic_slice(wd, (0, (1 - a) * half), (ff, half)), near)
    own_g = lax.dynamic_slice(wg, (a * half, 0), (half, ff))
    own_u = lax.dynamic_slice(wu, (a * half, 0), (half, ff))
    own_d = lax.dynamic_slice(wd, (0, a * half), (ff, half))
    pair_d = jnp.concatenate([own_d, got_d], axis=0)
    got_d2 = exchange(
        lax.dynamic_slice(pair_d, (0, (1 - b) * quarter), (2 * ff, quarter)), far
    )
    keep_d = lax.dynamic_slice(pair_d, (0, b * quarter), (2 * ff, quarter))

    column = jnp.arange(rows, dtype=jnp.int32)
    named = expert_ids[:, :, None] == (column // cap)[None, None, :]
    member = jnp.any(named, axis=1)
    weight = jnp.sum(jnp.where(named, gate_ints[:, :, None], 0), axis=1)
    below = jnp.arange(tok_rows)[:, None] > jnp.arange(tok_rows)[None, :]
    slot = jnp.dot(below.astype(BF16), member.astype(BF16), preferred_element_type=F32)
    placed = member & (slot == (column % cap).astype(F32)[None, :])
    place = placed.astype(BF16)
    weight = jnp.where(placed, weight, 0)
    low = weight % 16
    mixing = jnp.concatenate([(weight - low).astype(BF16), low.astype(BF16)], axis=0)

    tok_half = lax.dynamic_slice(tokens, (0, a * half), (tok_rows, half))
    outgoing = lax.dot_general(
        place, tok_half, (((0,), (0,)), ((), ())), preferred_element_type=F32
    ).astype(BF16)

    def all_to_all(x):
        width = x.shape[1]
        chunk = x.reshape(groups, cap * width // 128, 128)
        chunk = lax.all_to_all(chunk, "expert", 0, 0, tiled=True)
        return chunk.reshape(rows, width)

    arrived = all_to_all(outgoing)
    w_all = jnp.concatenate([own_g, own_u, got_g, got_u], axis=1)
    part = jnp.dot(arrived, w_all, preferred_element_type=F32)
    part_out = jnp.concatenate([part[:, 2 * ff :], part[:, : 2 * ff]], axis=1)
    full = part + exchange(part_out.astype(BF16), near).astype(F32)
    hidden = jnp.concatenate(
        [
            jax.nn.silu(full[:, :ff]) * full[:, ff : 2 * ff],
            jax.nn.silu(full[:, 2 * ff : 3 * ff]) * full[:, 3 * ff :],
        ],
        axis=1,
    ).astype(BF16)
    hidden = jnp.concatenate([hidden, exchange(hidden, far)], axis=1)
    down = jnp.concatenate([keep_d, got_d2], axis=0)
    partial = jnp.dot(hidden, down, preferred_element_type=F32).astype(BF16)

    back = all_to_all(partial)
    both = jnp.dot(mixing, back, preferred_element_type=F32)
    local = (both[:tok_rows] + both[tok_rows:]) * (1.0 / 1024.0)
    tiles = lax.all_gather(local.astype(BF16), "dp")
    tiles = tiles.reshape(n_dp // 4, 4, tok_rows, quarter).astype(F32).sum(axis=0)
    mixed = jnp.concatenate([tiles[0], tiles[2], tiles[1], tiles[3]], axis=1)
    return mixed.astype(BF16)


def solution(mesh):
    return jax.shard_map(
        on_device,
        mesh=mesh,
        in_specs=(
            P("expert", None),
            P("expert", None),
            P("expert", None),
            P("expert", None, "dp"),
            P("expert", None, "dp"),
            P("expert", "dp", None),
        ),
        out_specs=P("expert", None),
        check_vma=False,
    )
```

time: 340 us -> 164 us (0.48)
  waiting for transfers between devices: 158 us -> 49.1 us
  blocking collectives: 111 us -> 61.1 us
  starting transfers between devices: 5.97 us -> 37.8 us
  local copies, waits for them, and re-layouts: 30.5 us -> 8.76 us
  between operations: 13.5 us -> 0.32 us
  matrix products: 13.9 us -> 4.58 us
  other arithmetic: 6.61 us -> 1.63 us
    all_to_all x1, blocking collectives: 111 us -> 33.8 us  [all_to_all(): chunk = lax.all_to_all(chunk, 'expert', 0, 0, tiled=True)]
    all_to_all x1, waiting for transfers between devices: 95.6 us -> 29.9 us  [all_to_all(): chunk = lax.all_to_all(chunk, 'expert', 0, 0, tiled=True)]
    all_gather x1 -> x0, waiting for transfers between devices: 61.9 us -> none  [total_of_pieces(): tiles = lax.all_gather(value, axis).astype(jnp.float32)]
    all_gather x0 -> x1, blocking collectives: none -> 27.2 us  [on_device(): tiles = lax.all_gather(local.astype(BF16), 'dp')]
    ppermute x0 -> x6, starting transfers between devices: none -> 24.1 us  [exchange(): return lax.ppermute(x, ('dp', 'expert'), pairs)]
    ppermute x0 -> x6, waiting for transfers between devices: none -> 19.2 us  [exchange(): return lax.ppermute(x, ('dp', 'expert'), pairs)]
    reshape x5 -> x4, local copies, waits for them, and re-layouts: 22.9 us -> 4.88 us  [the longest x2 2.46 us: all_to_all(): chunk = x.reshape(groups, cap * width // 128, 128)]
    dot_general x3 -> x5, matrix products: 13.9 us -> 4.58 us  [the longest x1 2.97 us: on_device(): part = jnp.dot(arrived, w_all, preferred_element_type=F32)]
  transfers between devices with their start and end apart: 2 -> 7, of which waited for: 2 -> 3; matrix products, arithmetic and copies ran while one was open for 0% -> 5% of each run, Pallas kernels for 0% -> 0%
where the time goes in v1:
time: 164 us; the launch traced here: 163 us
  blocking collectives  61.1 us (37%)
  waiting for transfers between devices  49.1 us (30%)
  starting transfers between devices  37.8 us (23%)
  local copies, waits for them, and re-layouts  8.76 us (5%)
  matrix products  4.58 us (3%)
    all_to_all x1, blocking collectives, all_to_all(): chunk = lax.all_to_all(chunk, 'expert', 0, 0, tiled=True)  33.8 us
    all_to_all x1, waiting for transfers between devices, all_to_all(): chunk = lax.all_to_all(chunk, 'expert', 0, 0, tiled=True)  29.9 us
    all_gather x1, blocking collectives, on_device(): tiles = lax.all_gather(local.astype(BF16), 'dp')  27.2 us
    ppermute x6, starting transfers between devices, exchange(): return lax.ppermute(x, ('dp', 'expert'), pairs)  24.1 us
    ppermute x6, waiting for transfers between devices, exchange(): return lax.ppermute(x, ('dp', 'expert'), pairs)  19.2 us
    all_to_all x1, starting transfers between devices, all_to_all(): chunk = lax.all_to_all(chunk, 'expert', 0, 0, tiled=True)  13.8 us
  transfers between devices with their start and end apart: 7, of which 3 were waited for; matrix products, arithmetic and copies ran while one was open for 5% of the time, Pallas kernels for 0%

profile of v1, /device:TPU:2, one launch (start us, length us, event | category | flops | bytes accessed | tf_op | source)
XLA Modules:
  0.0 163.3 jit_solution(8217680839348502288)
XLA Ops:
  0.0 0.8 copy.9
  0.8 0.8 copy.10
  2.2 0.6 convolution_convert_fusion
  2.8 2.1 %reshape.46 = bf16[64,96,128]{2,1,0:T(8,128)(2,1)} reshape(bf16[384,2048]{1,0:T(8,128)(2,1)S(1)} %convolution_convert_fusion) | data formatting | bytes 3145728 | tf_op jit(solution)/shard_map/reshape | solution.py:69
  4.9 13.8 %all-to-all-start = ((bf16[64,96,128]{2,1,0:T(8,128)(2,1)}), bf16[64,96,128]{2,1,0:T(8,128)(2,1)S(1)}, u32[]{:S(2)}, u32[]{:S(2)}) async-start(bf16[64,96,128]{2,1,0:T(8,128)(2,1)} %reshape.46), calls=%async_computation | async-start | bytes 3145728 | tf_op jit(solution)/shard_map/all_to_all | solution.py:70
  18.7 1.1 dynamic-slice_bitcast_fusion.5
  19.8 2.0 %collective-permute-start = (bf16[2048,128]{1,0:T(8,128)(2,1)}, bf16[2048,128]{1,0:T(8,128)(2,1)}, u32[]{:S(2)}, u32[]{:S(2)}) collective-permute-start(bf16[2048,128]{1,0:T(8,128)(2,1)} %get-tuple-element.6), channel_id=1, source_target_pairs={{0,64},{1,705},{2,66},{3,707},{4,68},{5,709},{6,70},{7,711},{8,72}... | collective-permute-start | bytes 1572872 | tf_op jit(solution)/shard_map/ppermute | solution.py:21
  21.9 1.1 dynamic-slice_bitcast_fusion.4
  22.9 3.9 %collective-permute-start.1 = (bf16[2048,128]{1,0:T(8,128)(2,1)}, bf16[2048,128]{1,0:T(8,128)(2,1)}, u32[]{:S(2)}, u32[]{:S(2)}) collective-permute-start(bf16[2048,128]{1,0:T(8,128)(2,1)} %get-tuple-element.8), channel_id=1, source_target_pairs={{0,64},{1,705},{2,66},{3,707},{4,68},{5,709},{6,70},{7,711},{8,72}... | collective-permute-start | bytes 1572872 | tf_op jit(solution)/shard_map/ppermute | solution.py:21
  27.0 1.9 %collective-permute-start.4 = (bf16[128,2048]{1,0:T(8,128)(2,1)S(1)}, bf16[128,2048]{1,0:T(8,128)(2,1)S(1)}, u32[]{:S(2)}, u32[]{:S(2)}) collective-permute-start(bf16[128,2048]{1,0:T(8,128)(2,1)S(1)} %get-tuple-element.11), channel_id=1, source_target_pairs={{0,64},{1,705},{2,66},{3,707},{4,68},{5,709},{6,70},{7,711},{8,72}... | collective-permute-start | bytes 1572872 | tf_op jit(solution)/shard_map/ppermute | solution.py:21
  28.9 29.9 %all-to-all-done = bf16[64,96,128]{2,1,0:T(8,128)(2,1)S(1)} async-done(((bf16[64,96,128]{2,1,0:T(8,128)(2,1)}), bf16[64,96,128]{2,1,0:T(8,128)(2,1)S(1)}, u32[]{:S(2)}, u32[]{:S(2)}) %all-to-all-start) | async-done | bytes 1572896 | tf_op jit(solution)/shard_map/all_to_all | solution.py:70
  58.8 2.1 %reshape.47 = bf16[384,2048]{1,0:T(8,128)(2,1)} reshape(bf16[64,96,128]{2,1,0:T(8,128)(2,1)S(1)} %all-to-all-done) | data formatting | bytes 3145728 | tf_op jit(solution)/shard_map/reshape | solution.py:71
  60.9 3.0 %fusion.44 = (bf16[384,512]{1,0:T(8,128)(2,1)S(1)}, f32[384,512]{1,0:T(8,128)S(1)}) fusion(bf16[384,2048]{1,0:T(8,128)(2,1)} %reshape.47, bf16[2048,128]{1,0:T(8,128)(2,1)} %collective-permute-done.1, bf16[2048,128]{1,0:T(8,128)(2,1)} %collective-permute-done, bf16[2048,128]{1,0:T(8,128)(2,1)} %get-tuple-element.7, bf16[2048,128]{1,0:T(8,128)(2,1)} %get-tuple-element.5), kind=kOutput, calls=%fused_computation.79 | convolution fusion | flops 813891584 | bytes 4849664 | tf_op jit(solution)/shard_map/dot_general | solution.py:75
  63.9 1.9 %collective-permute-start.2 = (bf16[384,512]{1,0:T(8,128)(2,1)S(1)}, bf16[384,512]{1,0:T(8,128)(2,1)S(1)}, u32[]{:S(2)}, u32[]{:S(2)}) collective-permute-start(bf16[384,512]{1,0:T(8,128)(2,1)S(1)} %pad_maximum_fusion), channel_id=1, source_target_pairs={{0,64},{1,705},{2,66},{3,707},{4,68},{5,709},{6,70},{7,711},{8,72}... | collective-permute-start | bytes 1179656 | tf_op jit(solution)/shard_map/ppermute | solution.py:21
  66.0 5.4 %collective-permute-start.5 = (bf16[256,1024]{1,0:T(8,128)(2,1)S(1)}, bf16[256,1024]{1,0:T(8,128)(2,1)S(1)}, u32[]{:S(2)}, u32[]{:S(2)}) collective-permute-start(bf16[256,1024]{1,0:T(8,128)(2,1)S(1)} %get-tuple-element.10), channel_id=1, source_target_pairs={{0,128},{1,641},{2,130},{3,643},{4,132},{5,645},{6,134},{7,647},{8... | collective-permute-start | bytes 1572872 | tf_op jit(solution)/shard_map/ppermute | solution.py:21
  71.4 3.4 %collective-permute-done.2 = bf16[384,512]{1,0:T(8,128)(2,1)S(1)} collective-permute-done((bf16[384,512]{1,0:T(8,128)(2,1)S(1)}, bf16[384,512]{1,0:T(8,128)(2,1)S(1)}, u32[]{:S(2)}, u32[]{:S(2)}) %collective-permute-start.2) | collective-permute-done | bytes 393248 | tf_op jit(solution)/shard_map/ppermute | solution.py:21
  75.1 8.9 %collective-permute-start.3 = (bf16[384,256]{1,0:T(8,128)(2,1)S(1)}, bf16[384,256]{1,0:T(8,128)(2,1)S(1)}, u32[]{:S(2)}, u32[]{:S(2)}) collective-permute-start(bf16[384,256]{1,0:T(8,128)(2,1)S(1)} %pad_maximum_fusion.2), channel_id=1, source_target_pairs={{0,128},{1,641},{2,130},{3,643},{4,132},{5,645},{6,134},{7,647},{8... | collective-permute-start | bytes 589832 | tf_op jit(solution)/shard_map/ppermute | solution.py:21
  84.0 15.8 %collective-permute-done.3 = bf16[384,256]{1,0:T(8,128)(2,1)S(1)} collective-permute-done((bf16[384,256]{1,0:T(8,128)(2,1)S(1)}, bf16[384,256]{1,0:T(8,128)(2,1)S(1)}, u32[]{:S(2)}, u32[]{:S(2)}) %collective-permute-start.3) | collective-permute-done | bytes 196640 | tf_op jit(solution)/shard_map/ppermute | solution.py:21
  99.8 0.6 convolution_convert_fusion.1
  100.4 0.3 reshape.48
  100.7 33.8 %all_to_all.10 = bf16[64,48,128]{2,1,0:T(8,128)(2,1)S(1)} all-to-all(bf16[64,48,128]{2,1,0:T(8,128)(2,1)S(1)} %reshape.48), channel_id=1, replica_groups=mesh['dp'=12,'expert'=64] {'expert'}, dimensions={0} | all-to-all | bytes 1572864 | tf_op jit(solution)/shard_map/all_to_all | solution.py:70
  134.5 0.3 reshape.49
  135.2 27.2 %all-gather = bf16[384,1024]{1,0:T(8,128)(2,1)S(1)} all-gather(bf16[32,1024]{1,0:T(8,128)(2,1)S(1)} %fusion.23), channel_id=2, replica_groups=mesh['dp'=12,'expert'=64] {'dp'}, dimensions={0}, use_global_device_ids=true | all-gather | bytes 851968 | tf_op jit(solution)/shard_map/all_gather | solution.py:92
  162.6 0.7 pad_maximum_fusion.1
  (27 shorter events, 1.5 us)
Async XLA Ops:
  0.0 2.2 %copy-start = (bf16[32,4096]{1,0:T(8,128)(2,1)S(1)}, bf16[32,4096]{1,0:T(8,128)(2,1)}, u32[]{:S(2)}) copy-start(bf16[32,4096]{1,0:T(8,128)(2,1)} %param.6) | copy-start | bytes 786436
  4.9 13.8 %copy-start.1 = (bf16[1,4096,128]{2,1,0:T(8,128)(2,1)S(1)}, bf16[1,4096,128]{2,1,0:T(8,128)(2,1)}, u32[]{:S(2)}) copy-start(bf16[1,4096,128]{2,1,0:T(8,128)(2,1)} %param.9) | copy-start | bytes 3145732
  4.9 53.9 %all-to-all-start = ((bf16[64,96,128]{2,1,0:T(8,128)(2,1)}), bf16[64,96,128]{2,1,0:T(8,128)(2,1)S(1)}, u32[]{:S(2)}, u32[]{:S(2)}) async-start(bf16[64,96,128]{2,1,0:T(8,128)(2,1)} %reshape.46), calls=%async_computation | async-start | bytes 3145728 | tf_op jit(solution)/shard_map/all_to_all | solution.py:70
  18.7 3.1 %copy-start.2 = (bf16[1,4096,128]{2,1,0:T(8,128)(2,1)S(1)}, bf16[1,4096,128]{2,1,0:T(8,128)(2,1)}, u32[]{:S(2)}) copy-start(bf16[1,4096,128]{2,1,0:T(8,128)(2,1)} %param.10) | copy-start | bytes 3145732
  19.8 7.0 %copy-start.3 = (bf16[1,128,4096]{2,1,0:T(8,128)(2,1)S(1)}, bf16[1,128,4096]{2,1,0:T(8,128)(2,1)}, u32[]{:S(2)}) copy-start(bf16[1,128,4096]{2,1,0:T(8,128)(2,1)} %param.11) | copy-start | bytes 3145732
  19.8 41.1 %collective-permute-start = (bf16[2048,128]{1,0:T(8,128)(2,1)}, bf16[2048,128]{1,0:T(8,128)(2,1)}, u32[]{:S(2)}, u32[]{:S(2)}) collective-permute-start(bf16[2048,128]{1,0:T(8,128)(2,1)} %get-tuple-element.6), channel_id=1, source_target_pairs={{0,64},{1,705},{2,66},{3,707},{4,68},{5,709},{6,70},{7,711},{8,72}... | collective-permute-start | bytes 1572872 | tf_op jit(solution)/shard_map/ppermute | solution.py:21
  22.9 38.0 %collective-permute-start.1 = (bf16[2048,128]{1,0:T(8,128)(2,1)}, bf16[2048,128]{1,0:T(8,128)(2,1)}, u32[]{:S(2)}, u32[]{:S(2)}) collective-permute-start(bf16[2048,128]{1,0:T(8,128)(2,1)} %get-tuple-element.8), channel_id=1, source_target_pairs={{0,64},{1,705},{2,66},{3,707},{4,68},{5,709},{6,70},{7,711},{8,72}... | collective-permute-start | bytes 1572872 | tf_op jit(solution)/shard_map/ppermute | solution.py:21
  27.0 38.9 %collective-permute-start.4 = (bf16[128,2048]{1,0:T(8,128)(2,1)S(1)}, bf16[128,2048]{1,0:T(8,128)(2,1)S(1)}, u32[]{:S(2)}, u32[]{:S(2)}) collective-permute-start(bf16[128,2048]{1,0:T(8,128)(2,1)S(1)} %get-tuple-element.11), channel_id=1, source_target_pairs={{0,64},{1,705},{2,66},{3,707},{4,68},{5,709},{6,70},{7,711},{8,72}... | collective-permute-start | bytes 1572872 | tf_op jit(solution)/shard_map/ppermute | solution.py:21
  63.9 10.8 %collective-permute-start.2 = (bf16[384,512]{1,0:T(8,128)(2,1)S(1)}, bf16[384,512]{1,0:T(8,128)(2,1)S(1)}, u32[]{:S(2)}, u32[]{:S(2)}) collective-permute-start(bf16[384,512]{1,0:T(8,128)(2,1)S(1)} %pad_maximum_fusion), channel_id=1, source_target_pairs={{0,64},{1,705},{2,66},{3,707},{4,68},{5,709},{6,70},{7,711},{8,72}... | collective-permute-start | bytes 1179656 | tf_op jit(solution)/shard_map/ppermute | solution.py:21
  66.0 18.0 %collective-permute-start.5 = (bf16[256,1024]{1,0:T(8,128)(2,1)S(1)}, bf16[256,1024]{1,0:T(8,128)(2,1)S(1)}, u32[]{:S(2)}, u32[]{:S(2)}) collective-permute-start(bf16[256,1024]{1,0:T(8,128)(2,1)S(1)} %get-tuple-element.10), channel_id=1, source_target_pairs={{0,128},{1,641},{2,130},{3,643},{4,132},{5,645},{6,134},{7,647},{8... | collective-permute-start | bytes 1572872 | tf_op jit(solution)/shard_map/ppermute | solution.py:21
  75.1 24.7 %collective-permute-start.3 = (bf16[384,256]{1,0:T(8,128)(2,1)S(1)}, bf16[384,256]{1,0:T(8,128)(2,1)S(1)}, u32[]{:S(2)}, u32[]{:S(2)}) collective-permute-start(bf16[384,256]{1,0:T(8,128)(2,1)S(1)} %pad_maximum_fusion.2), channel_id=1, source_target_pairs={{0,128},{1,641},{2,130},{3,643},{4,132},{5,645},{6,134},{7,647},{8... | collective-permute-start | bytes 589832 | tf_op jit(solution)/shard_map/ppermute | solution.py:21

commit v2 on v1

v2 whole, which is shorter than its diff:
```python
import jax
import jax.numpy as jnp
from jax import lax
from jax.sharding import PartitionSpec as P

BF16 = jnp.bfloat16
F32 = jnp.float32


def partner_pairs(n_dp, n_expert, step):
    pairs = []
    for p in range(n_dp):
        for e in range(n_expert):
            shift = e % 2
            other = ((((p - shift) % n_dp) ^ step) + shift) % n_dp
            pairs.append((p * n_expert + e, other * n_expert + e))
    return pairs


def exchange(x, pairs):
    return lax.ppermute(x, ("dp", "expert"), pairs)


def on_device(tokens, expert_ids, gate_ints, w_gate, w_up, w_down):
    n_dp, groups = lax.axis_size("dp"), lax.axis_size("expert")
    tok_rows, feature = tokens.shape
    top = expert_ids.shape[1]
    cap = min(tok_rows, max(2, 3 * tok_rows * top // (2 * groups)))
    rows = groups * cap
    half, quarter = feature // 2, feature // 4
    ff = w_gate.shape[2]
    p, e = lax.axis_index("dp"), lax.axis_index("expert")
    shift = e % 2
    place_in_quad = jnp.mod(p - shift, n_dp)
    first = place_in_quad % 2 == 0

    def plane(step):
        return jnp.mod((place_in_quad ^ step) + shift, n_dp)

    def half_of(q):
        return (q % 2) * half

    def quarter_of(q):
        return half_of(q) + ((q // 2) % 2) * quarter

    near = partner_pairs(n_dp, groups, 1)
    far = partner_pairs(n_dp, groups, 2)
    cross = partner_pairs(n_dp, groups, 3)

    ids, ints = expert_ids.T, gate_ints.T
    row = jnp.arange(rows, dtype=jnp.int32)[:, None]
    named = ids[:, None, :] == (row // cap)[None, :, :]
    member = jnp.any(named, axis=0)
    weight = jnp.sum(jnp.where(named, ints[:, None, :], 0), axis=0)
    above = jnp.arange(tok_rows)[:, None] < jnp.arange(tok_rows)[None, :]
    slot = jnp.dot(member.astype(BF16), above.astype(BF16), preferred_element_type=F32)
    placed = member & (slot == (row % cap).astype(F32))
    place = placed.astype(BF16)
    weight = jnp.where(placed, weight, 0)
    low = weight % 16
    mixing = jnp.concatenate([(weight - low).astype(BF16), low.astype(BF16)], axis=1)

    tok_half = lax.dynamic_slice(tokens, (0, half_of(p)), (tok_rows, half))
    outgoing = jnp.dot(place, tok_half, preferred_element_type=F32).astype(BF16)

    def all_to_all(x):
        width = x.shape[1]
        chunk = x.reshape(groups, cap * width // 128, 128)
        chunk = lax.all_to_all(chunk, "expert", 0, 0, tiled=True)
        return chunk.reshape(rows, width)

    arrived = all_to_all(outgoing)

    wg, wu, wd = w_gate[0], w_up[0], w_down[0]
    q_near, q_far, q_cross = plane(1), plane(2), plane(3)
    got_g = exchange(lax.dynamic_slice(wg, (half_of(q_near), 0), (half, ff)), near)
    got_u = exchange(lax.dynamic_slice(wu, (half_of(q_near), 0), (half, ff)), near)
    own_g = lax.dynamic_slice(wg, (half_of(p), 0), (half, ff))
    own_u = lax.dynamic_slice(wu, (half_of(p), 0), (half, ff))
    own_d, for_near, for_far, for_cross = [
        lax.dynamic_slice(wd, (0, quarter_of(q)), (ff, quarter))
        for q in (p, q_near, q_far, q_cross)
    ]
    got_near = exchange(for_near, near)
    got_far = exchange(for_far, far)
    got_cross = exchange(for_cross, cross)

    def in_order(mine, other, axis):
        return jnp.concatenate(
            [jnp.where(first, mine, other), jnp.where(first, other, mine)], axis=axis
        )

    up_down = in_order(
        jnp.concatenate([own_g, own_u], axis=1), jnp.concatenate([got_g, got_u], axis=1), 1
    )
    down = jnp.concatenate(
        [in_order(own_d, got_near, 0), in_order(got_far, got_cross, 0)], axis=0
    )
    arrived, up_down, down = lax.optimization_barrier((arrived, up_down, down))

    part = jnp.dot(arrived, up_down, preferred_element_type=F32)
    full = part + exchange(part.astype(BF16), near).astype(F32)
    hidden = jnp.concatenate(
        [
            jax.nn.silu(full[:, :ff]) * full[:, ff : 2 * ff],
            jax.nn.silu(full[:, 2 * ff : 3 * ff]) * full[:, 3 * ff :],
        ],
        axis=1,
    ).astype(BF16)
    hidden = jnp.concatenate([hidden, exchange(hidden, far)], axis=1)
    partial = jnp.dot(hidden, down, preferred_element_type=F32).astype(BF16)

    back = all_to_all(partial)
    both = lax.dot_general(
        mixing, back, (((0,), (0,)), ((), ())), preferred_element_type=F32
    )
    local = (both[:tok_rows] + both[tok_rows:]) * (1.0 / 1024.0)
    tiles = lax.all_gather(local.astype(BF16), "dp")
    tiles = tiles.reshape(n_dp // 4, 4, tok_rows, quarter).astype(F32).sum(axis=0)
    mixed = jnp.concatenate([tiles[0], tiles[2], tiles[1], tiles[3]], axis=1)
    return mixed.astype(BF16)


def solution(mesh):
    return jax.shard_map(
        on_device,
        mesh=mesh,
        in_specs=(
            P("expert", None),
            P("expert", None),
            P("expert", None),
            P("expert", None, "dp"),
            P("expert", None, "dp"),
            P("expert", "dp", None),
        ),
        out_specs=P("expert", None),
        check_vma=False,
    )
```

time: 164 us -> 152 us (0.927)
  waiting for transfers between devices: 49.1 us -> 25.6 us
  other arithmetic: 1.63 us -> 8.04 us
  blocking collectives: 61.1 us -> 66.8 us
    all_to_all x1, waiting for transfers between devices: 29.9 us -> 4.2 us  [all_to_all(): chunk = lax.all_to_all(chunk, 'expert', 0, 0, tiled=True)]
    all_to_all x1, blocking collectives: 33.8 us -> 40.1 us  [all_to_all(): chunk = lax.all_to_all(chunk, 'expert', 0, 0, tiled=True)]
    select_n x1 -> x4, other arithmetic: 0.01 us -> 2.66 us  [the longest x3 2.65 us: in_order(): jnp.where(first, mine, other)]
    concatenate x2, other arithmetic: 0.11 us -> 2.55 us  [the longest x1 1.5 us: in_order(): jnp.concatenate([jnp.where(first, mine, other), jnp.where(first, other, m...]
    ppermute x6 -> x7, waiting for transfers between devices: 19.2 us -> 21.4 us  [exchange(): return lax.ppermute(x, ('dp', 'expert'), pairs)]
    dynamic_slice x3, local copies, waits for them, and re-layouts: 2.25 us -> 3.96 us  [the longest x1 2.15 us: on_device(): own_g = lax.dynamic_slice(wg, (half_of(p), 0), (half, ff))]
    ppermute x6 -> x7, starting transfers between devices: 24.1 us -> 23.5 us  [exchange(): return lax.ppermute(x, ('dp', 'expert'), pairs)]
  transfers between devices with their start and end apart: 7 -> 8, of which waited for: 3 -> 6; matrix products, arithmetic and copies ran while one was open for 5% -> 7% of each run, Pallas kernels for 0% -> 0%
where the time goes in v2:
time: 152 us; the launch traced here: 151 us
  blocking collectives  66.8 us (44%)
  starting transfers between devices  37.3 us (25%)
  waiting for transfers between devices  25.6 us (17%)
  local copies, waits for them, and re-layouts  8.74 us (6%)
  other arithmetic  8.04 us (5%)
  matrix products  4.25 us (3%)
    all_to_all x1, blocking collectives, all_to_all(): chunk = lax.all_to_all(chunk, 'expert', 0, 0, tiled=True)  40.1 us
    all_gather x1, blocking collectives, on_device(): tiles = lax.all_gather(local.astype(BF16), 'dp')  26.7 us
    ppermute x7, starting transfers between devices, exchange(): return lax.ppermute(x, ('dp', 'expert'), pairs)  23.5 us
    ppermute x7, waiting for transfers between devices, exchange(): return lax.ppermute(x, ('dp', 'expert'), pairs)  21.4 us
    all_to_all x1, starting transfers between devices, all_to_all(): chunk = lax.all_to_all(chunk, 'expert', 0, 0, tiled=True)  13.8 us
    all_to_all x1, waiting for transfers between devices, all_to_all(): chunk = lax.all_to_all(chunk, 'expert', 0, 0, tiled=True)  4.2 us
  transfers between devices with their start and end apart: 8, of which 6 were waited for; matrix products, arithmetic and copies ran while one was open for 7% of the time, Pallas kernels for 0%

profile of v2, /device:TPU:2, one launch (start us, length us, event | category | flops | bytes accessed | tf_op | source)
XLA Modules:
  0.0 151.3 jit_solution(8726546754464423893)
XLA Ops:
  2.6 2.1 %reshape.66 = bf16[64,96,128]{2,1,0:T(8,128)(2,1)} reshape(bf16[384,2048]{1,0:T(8,128)(2,1)S(1)} %convolution_convert_fusion) | data formatting | bytes 3145728 | tf_op jit(solution)/shard_map/reshape | solution.py:68
  4.7 13.8 %all-to-all-start = ((bf16[64,96,128]{2,1,0:T(8,128)(2,1)}), bf16[64,96,128]{2,1,0:T(8,128)(2,1)S(1)}, u32[]{:S(2)}, u32[]{:S(2)}) async-start(bf16[64,96,128]{2,1,0:T(8,128)(2,1)} %reshape.66), calls=%async_computation | async-start | bytes 3145728 | tf_op jit(solution)/shard_map/all_to_all | solution.py:69
  19.6 3.1 %collective-permute-start.3 = (bf16[128,1024]{1,0:T(8,128)(2,1)}, bf16[128,1024]{1,0:T(8,128)(2,1)}, u32[]{:S(2)}, u32[]{:S(2)}) collective-permute-start(bf16[128,1024]{1,0:T(8,128)(2,1)} %get-tuple-element.17), channel_id=1, source_target_pairs={{0,128},{1,641},{2,130},{3,643},{4,132},{5,645},{6,134},{7,647},{8... | collective-permute-start | bytes 786440 | tf_op jit(solution)/shard_map/ppermute | solution.py:21
  22.8 3.7 %collective-permute-start.4 = (bf16[128,1024]{1,0:T(8,128)(2,1)}, bf16[128,1024]{1,0:T(8,128)(2,1)}, u32[]{:S(2)}, u32[]{:S(2)}) collective-permute-start(bf16[128,1024]{1,0:T(8,128)(2,1)} %get-tuple-element.16), channel_id=1, source_target_pairs={{0,192},{1,577},{2,194},{3,579},{4,196},{5,581},{6,198},{7,583},{8... | collective-permute-start | bytes 786440 | tf_op jit(solution)/shard_map/ppermute | solution.py:21
  26.5 2.2 %dynamic-slice_bitcast_fusion.3 = (bf16[2048,128]{1,0:T(8,128)(2,1)S(1)}, bf16[2048,128]{1,0:T(8,128)(2,1)}) fusion(bf16[1,4096,128]{2,1,0:T(8,128)(2,1)} %param.9, s32[]{:T(128)S(6)} %select_n.177, s32[]{:T(128)S(6)} %select_n.184), kind=kLoop, calls=%fused_computation.13 | loop fusion | bytes 2097160 | tf_op jit(solution)/shard_map/dynamic_slice | solution.py:78
  28.7 2.5 %collective-permute-start = (bf16[2048,128]{1,0:T(8,128)(2,1)}, bf16[2048,128]{1,0:T(8,128)(2,1)S(1)}, u32[]{:S(2)}, u32[]{:S(2)}) collective-permute-start(bf16[2048,128]{1,0:T(8,128)(2,1)} %get-tuple-element.19), channel_id=1, source_target_pairs={{0,64},{1,705},{2,66},{3,707},{4,68},{5,709},{6,70},{7,711},{8,72}... | collective-permute-start | bytes 1572872 | tf_op jit(solution)/shard_map/ppermute | solution.py:21
  31.1 3.4 %collective-permute-start.2 = (bf16[128,1024]{1,0:T(8,128)(2,1)}, bf16[128,1024]{1,0:T(8,128)(2,1)}, u32[]{:S(2)}, u32[]{:S(2)}) collective-permute-start(bf16[128,1024]{1,0:T(8,128)(2,1)} %get-tuple-element.15), channel_id=1, source_target_pairs={{0,64},{1,705},{2,66},{3,707},{4,68},{5,709},{6,70},{7,711},{8,72}... | collective-permute-start | bytes 786440 | tf_op jit(solution)/shard_map/ppermute | solution.py:21
  35.4 2.5 %collective-permute-start.1 = (bf16[2048,128]{1,0:T(8,128)(2,1)}, bf16[2048,128]{1,0:T(8,128)(2,1)}, u32[]{:S(2)}, u32[]{:S(2)}) collective-permute-start(bf16[2048,128]{1,0:T(8,128)(2,1)} %get-tuple-element.21), channel_id=1, source_target_pairs={{0,64},{1,705},{2,66},{3,707},{4,68},{5,709},{6,70},{7,711},{8,72}... | collective-permute-start | bytes 1572872 | tf_op jit(solution)/shard_map/ppermute | solution.py:21
  37.9 4.9 %collective-permute-done.4 = bf16[128,1024]{1,0:T(8,128)(2,1)} collective-permute-done((bf16[128,1024]{1,0:T(8,128)(2,1)}, bf16[128,1024]{1,0:T(8,128)(2,1)}, u32[]{:S(2)}, u32[]{:S(2)}) %collective-permute-start.4) | collective-permute-done | bytes 262176 | tf_op jit(solution)/shard_map/ppermute | solution.py:21
  42.9 1.1 broadcast_select_fusion.3
  44.0 1.7 %collective-permute-done.2 = bf16[128,1024]{1,0:T(8,128)(2,1)} collective-permute-done((bf16[128,1024]{1,0:T(8,128)(2,1)}, bf16[128,1024]{1,0:T(8,128)(2,1)}, u32[]{:S(2)}, u32[]{:S(2)}) %collective-permute-start.2) | collective-permute-done | bytes 262176 | tf_op jit(solution)/shard_map/ppermute | solution.py:21
  45.7 1.1 bitcast_select_fusion.1
  46.8 1.1 pad_maximum_fusion.2
  48.0 3.3 %collective-permute-done.1 = bf16[2048,128]{1,0:T(8,128)(2,1)} collective-permute-done((bf16[2048,128]{1,0:T(8,128)(2,1)}, bf16[2048,128]{1,0:T(8,128)(2,1)}, u32[]{:S(2)}, u32[]{:S(2)}) %collective-permute-start.1) | collective-permute-done | bytes 524320 | tf_op jit(solution)/shard_map/ppermute | solution.py:21
  51.3 1.2 constant_dynamic-update-slice_fusion
  52.9 1.5 pad_maximum_fusion
  54.4 4.2 %all-to-all-done = bf16[64,96,128]{2,1,0:T(8,128)(2,1)S(1)} async-done(((bf16[64,96,128]{2,1,0:T(8,128)(2,1)}), bf16[64,96,128]{2,1,0:T(8,128)(2,1)S(1)}, u32[]{:S(2)}, u32[]{:S(2)}) %all-to-all-start) | async-done | bytes 1572896 | tf_op jit(solution)/shard_map/all_to_all | solution.py:69
  59.3 2.6 %fusion.29 = (bf16[384,512]{1,0:T(8,128)(2,1)S(1)}, f32[384,512]{1,0:T(8,128)S(1)}) fusion(bf16[384,2048]{1,0:T(8,128)(2,1)S(1)} %reshape.67, bf16[2048,512]{1,0:T(8,128)(2,1)} %pad_maximum_fusion), kind=kOutput, calls=%fused_computation.71 | convolution fusion | flops 805502976 | bytes 4849664 | tf_op jit(solution)/shard_map/dot_general | solution.py:101
  61.9 2.1 %collective-permute-start.5 = (bf16[384,512]{1,0:T(8,128)(2,1)S(1)}, bf16[384,512]{1,0:T(8,128)(2,1)S(1)}, u32[]{:S(2)}, u32[]{:S(2)}) collective-permute-start(bf16[384,512]{1,0:T(8,128)(2,1)S(1)} %get-tuple-element.32), channel_id=1, source_target_pairs={{0,64},{1,705},{2,66},{3,707},{4,68},{5,709},{6,70},{7,711},{8,72}... | collective-permute-start | bytes 1179656 | tf_op jit(solution)/shard_map/ppermute | solution.py:21
  64.0 7.7 %collective-permute-done.5 = bf16[384,512]{1,0:T(8,128)(2,1)S(1)} collective-permute-done((bf16[384,512]{1,0:T(8,128)(2,1)S(1)}, bf16[384,512]{1,0:T(8,128)(2,1)S(1)}, u32[]{:S(2)}, u32[]{:S(2)}) %collective-permute-start.5) | collective-permute-done | bytes 393248 | tf_op jit(solution)/shard_map/ppermute | solution.py:21
  72.0 6.4 %collective-permute-start.6 = (bf16[384,256]{1,0:T(8,128)(2,1)S(1)}, bf16[384,256]{1,0:T(8,128)(2,1)S(1)}, u32[]{:S(2)}, u32[]{:S(2)}) collective-permute-start(bf16[384,256]{1,0:T(8,128)(2,1)S(1)} %pad_maximum_fusion.4), channel_id=1, source_target_pairs={{0,128},{1,641},{2,130},{3,643},{4,132},{5,645},{6,134},{7,647},{8... | collective-permute-start | bytes 589832 | tf_op jit(solution)/shard_map/ppermute | solution.py:21
  78.4 3.7 %collective-permute-done.6 = bf16[384,256]{1,0:T(8,128)(2,1)S(1)} collective-permute-done((bf16[384,256]{1,0:T(8,128)(2,1)S(1)}, bf16[384,256]{1,0:T(8,128)(2,1)S(1)}, u32[]{:S(2)}, u32[]{:S(2)}) %collective-permute-start.6) | collective-permute-done | bytes 196640 | tf_op jit(solution)/shard_map/ppermute | solution.py:21
  83.0 40.1 %all_to_all.10 = bf16[64,48,128]{2,1,0:T(8,128)(2,1)S(1)} all-to-all(bf16[64,48,128]{2,1,0:T(8,128)(2,1)S(1)} %reshape.68), channel_id=1, replica_groups=mesh['dp'=12,'expert'=64] {'expert'}, dimensions={0} | all-to-all | bytes 1572864 | tf_op jit(solution)/shard_map/all_to_all | solution.py:69
  123.7 26.7 %all-gather = bf16[384,1024]{1,0:T(8,128)(2,1)S(1)} all-gather(bf16[32,1024]{1,0:T(8,128)(2,1)S(1)} %fusion.10), channel_id=2, replica_groups=mesh['dp'=12,'expert'=64] {'dp'}, dimensions={0}, use_global_device_ids=true | all-gather | bytes 851968 | tf_op jit(solution)/shard_map/all_gather | solution.py:118
  (31 shorter events, 8.3 us)
Async XLA Ops:
  0.0 2.0 %copy-start = (bf16[32,4096]{1,0:T(8,128)(2,1)S(1)}, bf16[32,4096]{1,0:T(8,128)(2,1)}, u32[]{:S(2)}) copy-start(bf16[32,4096]{1,0:T(8,128)(2,1)} %param.6) | copy-start | bytes 786436
  4.7 14.0 %copy-start.1 = (bf16[1,128,4096]{2,1,0:T(8,128)(2,1)S(1)}, bf16[1,128,4096]{2,1,0:T(8,128)(2,1)}, u32[]{:S(2)}) copy-start(bf16[1,128,4096]{2,1,0:T(8,128)(2,1)} %param.11) | copy-start | bytes 3145732
  4.7 53.9 %all-to-all-start = ((bf16[64,96,128]{2,1,0:T(8,128)(2,1)}), bf16[64,96,128]{2,1,0:T(8,128)(2,1)S(1)}, u32[]{:S(2)}, u32[]{:S(2)}) async-start(bf16[64,96,128]{2,1,0:T(8,128)(2,1)} %reshape.66), calls=%async_computation | async-start | bytes 3145728 | tf_op jit(solution)/shard_map/all_to_all | solution.py:69
  19.6 18.3 %collective-permute-start.3 = (bf16[128,1024]{1,0:T(8,128)(2,1)}, bf16[128,1024]{1,0:T(8,128)(2,1)}, u32[]{:S(2)}, u32[]{:S(2)}) collective-permute-start(bf16[128,1024]{1,0:T(8,128)(2,1)} %get-tuple-element.17), channel_id=1, source_target_pairs={{0,128},{1,641},{2,130},{3,643},{4,132},{5,645},{6,134},{7,647},{8... | collective-permute-start | bytes 786440 | tf_op jit(solution)/shard_map/ppermute | solution.py:21
  22.8 20.1 %collective-permute-start.4 = (bf16[128,1024]{1,0:T(8,128)(2,1)}, bf16[128,1024]{1,0:T(8,128)(2,1)}, u32[]{:S(2)}, u32[]{:S(2)}) collective-permute-start(bf16[128,1024]{1,0:T(8,128)(2,1)} %get-tuple-element.16), channel_id=1, source_target_pairs={{0,192},{1,577},{2,194},{3,579},{4,196},{5,581},{6,198},{7,583},{8... | collective-permute-start | bytes 786440 | tf_op jit(solution)/shard_map/ppermute | solution.py:21
  26.5 8.0 %copy-start.3 = (bf16[1,4096,128]{2,1,0:T(8,128)(2,1)S(1)}, bf16[1,4096,128]{2,1,0:T(8,128)(2,1)}, u32[]{:S(2)}) copy-start(bf16[1,4096,128]{2,1,0:T(8,128)(2,1)} %param.10) | copy-start | bytes 3145732
  28.7 19.2 %collective-permute-start = (bf16[2048,128]{1,0:T(8,128)(2,1)}, bf16[2048,128]{1,0:T(8,128)(2,1)S(1)}, u32[]{:S(2)}, u32[]{:S(2)}) collective-permute-start(bf16[2048,128]{1,0:T(8,128)(2,1)} %get-tuple-element.19), channel_id=1, source_target_pairs={{0,64},{1,705},{2,66},{3,707},{4,68},{5,709},{6,70},{7,711},{8,72}... | collective-permute-start | bytes 1572872 | tf_op jit(solution)/shard_map/ppermute | solution.py:21
  31.1 14.5 %collective-permute-start.2 = (bf16[128,1024]{1,0:T(8,128)(2,1)}, bf16[128,1024]{1,0:T(8,128)(2,1)}, u32[]{:S(2)}, u32[]{:S(2)}) collective-permute-start(bf16[128,1024]{1,0:T(8,128)(2,1)} %get-tuple-element.15), channel_id=1, source_target_pairs={{0,64},{1,705},{2,66},{3,707},{4,68},{5,709},{6,70},{7,711},{8,72}... | collective-permute-start | bytes 786440 | tf_op jit(solution)/shard_map/ppermute | solution.py:21
  35.4 15.9 %collective-permute-start.1 = (bf16[2048,128]{1,0:T(8,128)(2,1)}, bf16[2048,128]{1,0:T(8,128)(2,1)}, u32[]{:S(2)}, u32[]{:S(2)}) collective-permute-start(bf16[2048,128]{1,0:T(8,128)(2,1)} %get-tuple-element.21), channel_id=1, source_target_pairs={{0,64},{1,705},{2,66},{3,707},{4,68},{5,709},{6,70},{7,711},{8,72}... | collective-permute-start | bytes 1572872 | tf_op jit(solution)/shard_map/ppermute | solution.py:21
  61.9 20.2 %copy-start.2 = (bf16[512,1024]{1,0:T(8,128)(2,1)S(1)}, bf16[512,1024]{1,0:T(8,128)(2,1)}, u32[]{:S(2)}) copy-start(bf16[512,1024]{1,0:T(8,128)(2,1)} %pad_maximum_fusion.2) | copy-start | bytes 3145732
  61.9 9.8 %collective-permute-start.5 = (bf16[384,512]{1,0:T(8,128)(2,1)S(1)}, bf16[384,512]{1,0:T(8,128)(2,1)S(1)}, u32[]{:S(2)}, u32[]{:S(2)}) collective-permute-start(bf16[384,512]{1,0:T(8,128)(2,1)S(1)} %get-tuple-element.32), channel_id=1, source_target_pairs={{0,64},{1,705},{2,66},{3,707},{4,68},{5,709},{6,70},{7,711},{8,72}... | collective-permute-start | bytes 1179656 | tf_op jit(solution)/shard_map/ppermute | solution.py:21
  72.0 10.1 %collective-permute-start.6 = (bf16[384,256]{1,0:T(8,128)(2,1)S(1)}, bf16[384,256]{1,0:T(8,128)(2,1)S(1)}, u32[]{:S(2)}, u32[]{:S(2)}) collective-permute-start(bf16[384,256]{1,0:T(8,128)(2,1)S(1)} %pad_maximum_fusion.4), channel_id=1, source_target_pairs={{0,128},{1,641},{2,130},{3,643},{4,132},{5,645},{6,134},{7,647},{8... | collective-permute-start | bytes 589832 | tf_op jit(solution)/shard_map/ppermute | solution.py:21

commit v3 on v1

v3 whole, which is shorter than its diff:
```python
import functools

import jax
import jax.numpy as jnp
from jax import lax
from jax.experimental import pallas as pl
from jax.experimental.pallas import tpu as pltpu
from jax.sharding import PartitionSpec as P

BF16 = jnp.bfloat16
F32 = jnp.float32


def near_of(p, core, n_dp):
    return ((p - core) % n_dp ^ 1) + core


def far_of(p, core, n_dp):
    return near_of(p, 1 - core, n_dp)


def pairs_of(n_dp, n_expert, target):
    pairs = []
    for p in range(n_dp):
        for e in range(n_expert):
            pairs.append((p * n_expert + e, target(p, e % 2) % n_dp * n_expert + e))
    return pairs


def exchange(x, pairs):
    return lax.ppermute(x, ("dp", "expert"), pairs)


def place_rows(cap, ids_ref, tok_ref, out_ref, used):
    top, tok_rows = ids_ref.shape

    def clear(i, carry):
        out_ref[i] = jnp.zeros(out_ref.shape[1:], out_ref.dtype)
        return carry

    lax.fori_loop(0, out_ref.shape[0], clear, 0, unroll=16)
    for e in range(used.shape[0]):
        used[e] = 0

    def one(t, carry):
        row = tok_ref[t]
        experts = [ids_ref[k, t] for k in range(top)]
        slots = [used[e] for e in experts]
        for e, slot in zip(experts, slots):
            out_ref[e * cap + slot] = row
            used[e] = slot + 1
        return carry

    lax.fori_loop(0, tok_rows, one, 0, unroll=4)


def dispatch_rows(ids, tok, groups, cap):
    return pl.pallas_call(
        functools.partial(place_rows, cap),
        out_shape=jax.ShapeDtypeStruct((groups * cap,) + tok.shape[1:], tok.dtype),
        in_specs=[
            pl.BlockSpec(memory_space=pltpu.SMEM),
            pl.BlockSpec(memory_space=pltpu.VMEM),
        ],
        out_specs=pl.BlockSpec(memory_space=pltpu.VMEM),
        scratch_shapes=[pltpu.SMEM((groups,), jnp.int32)],
        name="place_rows",
    )(ids, tok)


def on_device(tokens, expert_ids, gate_ints, w_gate, w_up, w_down):
    n_dp, groups = lax.axis_size("dp"), lax.axis_size("expert")
    tok_rows, feature = tokens.shape
    top = expert_ids.shape[1]
    cap = min(tok_rows, max(2, 3 * tok_rows * top // (2 * groups)))
    rows = groups * cap
    half, quarter = feature // 2, feature // 4
    ff = w_gate.shape[2]
    p = lax.axis_index("dp")
    core = lax.axis_index("expert") % 2

    def near_plane(q):
        return (jnp.mod(q - core, n_dp) ^ 1) + core

    def far_plane(q):
        return (jnp.mod(q - 1 + core, n_dp) ^ 1) + 1 - core

    near = pairs_of(n_dp, groups, lambda q, c: near_of(q, c, n_dp))
    far = pairs_of(n_dp, groups, lambda q, c: far_of(q, c, n_dp))
    cross = pairs_of(
        n_dp, groups, lambda q, c: far_of(near_of(q, c, n_dp) % n_dp, c, n_dp)
    )

    tok_half = lax.dynamic_slice(tokens, (0, p % 2 * half), (tok_rows, half))
    outgoing = dispatch_rows(
        expert_ids.T, tok_half.reshape(tok_rows, half // 128, 128), groups, cap
    )

    def all_to_all(chunk, width):
        chunk = chunk.reshape(groups, cap * width // 128, 128)
        chunk = lax.all_to_all(chunk, "expert", 0, 0, tiled=True)
        return chunk.reshape(rows, width)

    arrived = all_to_all(outgoing, half)

    wg, wu, wd = w_gate[0], w_up[0], w_down[0]

    def down_for(q):
        return lax.dynamic_slice(wd, (0, jnp.mod(q, 4) * quarter), (ff, quarter))

    def gate_up_for(q):
        at = (q % 2 * half, 0)
        return jnp.concatenate(
            [lax.dynamic_slice(w, at, (half, ff)) for w in (wg, wu)], axis=1
        )

    folds = quarter // (2 * ff)
    q_near, q_far = jnp.mod(near_plane(p), n_dp), jnp.mod(far_plane(p), n_dp)
    q_cross = jnp.mod(far_plane(q_near), n_dp)
    for_near = down_for(q_near)
    folded = [for_near[:, i * 2 * ff : (i + 1) * 2 * ff] for i in range(folds)]
    got = exchange(jnp.concatenate([gate_up_for(q_near)] + folded, axis=0), near)
    got_far = exchange(down_for(q_far), far)
    got_cross = exchange(down_for(q_cross), cross)
    got_near = jnp.concatenate(
        [got[half + i * ff : half + (i + 1) * ff] for i in range(folds)], axis=1
    )
    down = jnp.concatenate([down_for(p), got_near, got_far, got_cross], axis=0)
    own_gu = gate_up_for(p)
    arrived, own_gu, got_gu, down, late_ids, late_ints = lax.optimization_barrier(
        (arrived, own_gu, got[:half], down, expert_ids, gate_ints)
    )

    mine = jnp.dot(arrived, own_gu, preferred_element_type=F32)
    theirs = jnp.dot(arrived, got_gu, preferred_element_type=F32)
    other = exchange(jnp.concatenate([mine, theirs], axis=1).astype(BF16), near)

    row = jnp.arange(rows, dtype=jnp.int32)[:, None]
    named = late_ids.T[:, None, :] == (row // cap)[None, :, :]
    member = jnp.any(named, axis=0)
    weight = jnp.sum(jnp.where(named, late_ints.T[:, None, :], 0), axis=0)
    above = jnp.arange(tok_rows)[:, None] < jnp.arange(tok_rows)[None, :]
    slot = jnp.dot(member.astype(BF16), above.astype(BF16), preferred_element_type=F32)
    weight = jnp.where(member & (slot == (row % cap).astype(F32)), weight, 0)
    low = weight % 16
    mixing = jnp.concatenate([(weight - low).astype(BF16), low.astype(BF16)], axis=1)
    other, mixing = lax.optimization_barrier((other, mixing))

    def act(x, y):
        z = x + y.astype(F32)
        return (jax.nn.silu(z[:, :ff]) * z[:, ff:]).astype(BF16)

    hidden = jnp.concatenate(
        [act(mine, other[:, 2 * ff :]), act(theirs, other[:, : 2 * ff])], axis=1
    )
    hidden = jnp.concatenate([hidden, exchange(hidden, far)], axis=1)
    partial = jnp.dot(hidden, down, preferred_element_type=F32).astype(BF16)

    back = all_to_all(partial, quarter)
    both = lax.dot_general(
        mixing, back, (((0,), (0,)), ((), ())), preferred_element_type=F32
    )
    local = (both[:tok_rows] + both[tok_rows:]) * (1.0 / 1024.0)
    tiles = lax.all_gather(local.astype(BF16), "dp")
    tiles = tiles.reshape(n_dp // 4, 4, tok_rows, quarter).astype(F32).sum(axis=0)
    mixed = jnp.concatenate([tiles[i] for i in range(4)], axis=1)
    return mixed.astype(BF16)


def solution(mesh):
    return jax.shard_map(
        on_device,
        mesh=mesh,
        in_specs=(
            P("expert", None),
            P("expert", None),
            P("expert", None),
            P("expert", None, "dp"),
            P("expert", None, "dp"),
            P("expert", "dp", None),
        ),
        out_specs=P("expert", None),
        check_vma=False,
    )
```

time: 164 us -> 147 us (0.90)
  waiting for transfers between devices: 49.1 us -> 29.2 us
  starting transfers between devices: 37.8 us -> 43.4 us
  blocking collectives: 61.1 us -> 56.1 us
  Pallas kernels: 0 us -> 3.49 us
  local copies, waits for them, and re-layouts: 8.76 us -> 5.99 us
  other arithmetic: 1.63 us -> 3.71 us
    all_to_all x1, waiting for transfers between devices: 29.9 us -> 0.01 us  [all_to_all(): chunk = lax.all_to_all(chunk, 'expert', 0, 0, tiled=True)]
    ppermute x6 -> x5, waiting for transfers between devices: 19.2 us -> 29.2 us  [exchange(): return lax.ppermute(x, ('dp', 'expert'), pairs)]
    ppermute x6 -> x5, starting transfers between devices: 24.1 us -> 29.8 us  [exchange(): return lax.ppermute(x, ('dp', 'expert'), pairs)]
    all_to_all x1, blocking collectives: 33.8 us -> 28.4 us  [all_to_all(): chunk = lax.all_to_all(chunk, 'expert', 0, 0, tiled=True)]
    pallas_call x0 -> x1, Pallas kernels: none -> 3.49 us  [dispatch_rows(): pl.pallas_call(functools.partial(place_rows, cap), out_shape=jax.ShapeDty...]
    reshape x2 -> x1, local copies, waits for them, and re-layouts: 2.46 us -> 0.33 us  [all_to_all(): chunk = chunk.reshape(groups, cap * width // 128, 128)]
    concatenate x4 -> x6, other arithmetic: 0.86 us -> 2.95 us  [the longest x1 1.09 us: gate_up_for(): jnp.concatenate([lax.dynamic_slice(w, at, (half, ff)) for w in (wg, wu)],...]
  transfers between devices with their start and end apart: 7 -> 6, of which waited for: 3 -> 4; matrix products, arithmetic and copies ran while one was open for 5% -> 4% of each run, Pallas kernels for 0% -> 0%
where the time goes in v3:
time: 147 us; the launch traced here: 146 us
  blocking collectives  56.1 us (38%)
  starting transfers between devices  43.4 us (30%)
  waiting for transfers between devices  29.2 us (20%)
  local copies, waits for them, and re-layouts  5.99 us (4%)
  matrix products  3.9 us (3%)
  other arithmetic  3.71 us (3%)
  Pallas kernels  3.49 us (2%)
    ppermute x5, starting transfers between devices, exchange(): return lax.ppermute(x, ('dp', 'expert'), pairs)  29.8 us
    ppermute x5, waiting for transfers between devices, exchange(): return lax.ppermute(x, ('dp', 'expert'), pairs)  29.2 us
    all_to_all x1, blocking collectives, all_to_all(): chunk = lax.all_to_all(chunk, 'expert', 0, 0, tiled=True)  28.4 us
    all_gather x1, blocking collectives, on_device(): tiles = lax.all_gather(local.astype(BF16), 'dp')  27.7 us
    all_to_all x1, starting transfers between devices, all_to_all(): chunk = lax.all_to_all(chunk, 'expert', 0, 0, tiled=True)  13.6 us
    pallas_call x1, Pallas kernels, dispatch_rows(): pl.pallas_call(functools.partial(place_rows, cap), out_shape=jax.ShapeDty...  3.49 us
  transfers between devices with their start and end apart: 6, of which 4 were waited for; matrix products, arithmetic and copies ran while one was open for 4% of the time, Pallas kernels for 0%

profile of v3, /device:TPU:2, one launch (start us, length us, event | category | flops | bytes accessed | tf_op | source)
XLA Modules:
  0.0 146.3 jit_solution(7782326626915581884)
XLA Ops:
  0.0 0.9 copy-done
  1.0 0.7 copy.7
  1.6 3.5 %place_rows.1 = bf16[384,16,128]{2,1,0:T(8,128)(2,1)} custom-call(s32[8,32]{1,0:T(8,128)} %bitcast.43, bf16[32,16,128]{2,1,0:T(8,128)(2,1)} %bitcast.42), custom_call_target="tpu_custom_call" | custom-call | tf_op jit(solution)/shard_map/place_rows/pallas_call | solution.py:58
  5.1 13.6 %all-to-all-start = ((bf16[64,96,128]{2,1,0:T(8,128)(2,1)}), bf16[64,96,128]{2,1,0:T(8,128)(2,1)S(1)}, u32[]{:S(2)}, u32[]{:S(2)}) async-start(bf16[64,96,128]{2,1,0:T(8,128)(2,1)} %bitcast.40), calls=%async_computation | async-start | bytes 3145728 | tf_op jit(solution)/shard_map/all_to_all | solution.py:101
  19.0 1.4 dynamic-slice_bitcast_fusion.6
  21.0 1.9 %collective-permute-start = (bf16[2560,256]{1,0:T(8,128)(2,1)S(1)}, bf16[2560,256]{1,0:T(8,128)(2,1)S(1)}, u32[]{:S(2)}, u32[]{:S(2)}) collective-permute-start(bf16[2560,256]{1,0:T(8,128)(2,1)S(1)} %slice_dynamic-update-slice_fusion), channel_id=1, source_target_pairs={{0,64},{1,705},{2,66},{3,707},{4,68},{5,709},{6,70},{7,711},{8,72}... | collective-permute-start | bytes 3932168 | tf_op jit(solution)/shard_map/ppermute | solution.py:31
  22.9 5.5 %collective-permute-start.2 = (bf16[128,1024]{1,0:T(8,128)(2,1)S(1)}, bf16[128,1024]{1,0:T(8,128)(2,1)S(1)}, u32[]{:S(2)}, u32[]{:S(2)}) collective-permute-start(bf16[128,1024]{1,0:T(8,128)(2,1)S(1)} %get-tuple-element.27), channel_id=1, source_target_pairs={{0,128},{1,641},{2,130},{3,643},{4,132},{5,645},{6,134},{7,647},{8... | collective-permute-start | bytes 786440 | tf_op jit(solution)/shard_map/ppermute | solution.py:31
  28.4 9.1 %collective-permute-start.1 = (bf16[128,1024]{1,0:T(8,128)(2,1)S(1)}, bf16[128,1024]{1,0:T(8,128)(2,1)S(1)}, u32[]{:S(2)}, u32[]{:S(2)}) collective-permute-start(bf16[128,1024]{1,0:T(8,128)(2,1)S(1)} %get-tuple-element.28), channel_id=1, source_target_pairs={{0,704},{1,65},{2,706},{3,67},{4,708},{5,69},{6,710},{7,71},{8,712... | collective-permute-start | bytes 786440 | tf_op jit(solution)/shard_map/ppermute | solution.py:31
  37.6 1.1 pad_maximum_fusion
  38.7 6.0 %collective-permute-done = bf16[2560,256]{1,0:T(8,128)(2,1)S(1)} collective-permute-done((bf16[2560,256]{1,0:T(8,128)(2,1)S(1)}, bf16[2560,256]{1,0:T(8,128)(2,1)S(1)}, u32[]{:S(2)}, u32[]{:S(2)}) %collective-permute-start) | collective-permute-done | bytes 1310752 | tf_op jit(solution)/shard_map/ppermute | solution.py:31
  44.7 1.1 slice.92
  45.8 12.3 %collective-permute-done.2 = bf16[128,1024]{1,0:T(8,128)(2,1)S(1)} collective-permute-done((bf16[128,1024]{1,0:T(8,128)(2,1)S(1)}, bf16[128,1024]{1,0:T(8,128)(2,1)S(1)}, u32[]{:S(2)}, u32[]{:S(2)}) %collective-permute-start.2) | collective-permute-done | bytes 262176 | tf_op jit(solution)/shard_map/ppermute | solution.py:31
  58.1 1.1 pad_maximum_fusion.1
  59.2 0.7 reshape.71
  59.9 2.1 %fusion.24 = (bf16[384,256]{0,1:T(8,128)(2,1)S(1)}, f32[384,256]{0,1:T(8,128)S(1)}) fusion(bf16[384,2048]{1,0:T(8,128)(2,1)S(1)} %reshape.71, bf16[2048,256]{1,0:T(8,128)(2,1)} %slice.92), kind=kOutput, calls=%fused_computation.66 | convolution fusion | flops 402751488 | bytes 3211264 | tf_op jit(solution)/shard_map/dot_general | solution.py:135
  62.0 0.8 fusion.25
  62.8 1.9 %collective-permute-start.3 = (bf16[384,512]{0,1:T(8,128)(2,1)S(1)}, bf16[384,512]{0,1:T(8,128)(2,1)S(1)}, u32[]{:S(2)}, u32[]{:S(2)}) collective-permute-start(bf16[384,512]{0,1:T(8,128)(2,1)S(1)} %pad_maximum_fusion.2), channel_id=1, source_target_pairs={{0,64},{1,705},{2,66},{3,707},{4,68},{5,709},{6,70},{7,711},{8,72}... | collective-permute-start | bytes 1179656 | tf_op jit(solution)/shard_map/ppermute | solution.py:31
  65.3 7.2 %collective-permute-done.3 = bf16[384,512]{0,1:T(8,128)(2,1)S(1)} collective-permute-done((bf16[384,512]{0,1:T(8,128)(2,1)S(1)}, bf16[384,512]{0,1:T(8,128)(2,1)S(1)}, u32[]{:S(2)}, u32[]{:S(2)}) %collective-permute-start.3) | collective-permute-done | bytes 393248 | tf_op jit(solution)/shard_map/ppermute | solution.py:31
  72.7 11.4 %collective-permute-start.4 = (bf16[384,256]{0,1:T(8,128)(2,1)S(1)}, bf16[384,256]{0,1:T(8,128)(2,1)S(1)}, u32[]{:S(2)}, u32[]{:S(2)}) collective-permute-start(bf16[384,256]{0,1:T(8,128)(2,1)S(1)} %pad_maximum_fusion.4), channel_id=1, source_target_pairs={{0,704},{1,65},{2,706},{3,67},{4,708},{5,69},{6,710},{7,71},{8,712... | collective-permute-start | bytes 589832 | tf_op jit(solution)/shard_map/ppermute | solution.py:31
  84.1 3.6 %collective-permute-done.4 = bf16[384,256]{0,1:T(8,128)(2,1)S(1)} collective-permute-done((bf16[384,256]{0,1:T(8,128)(2,1)S(1)}, bf16[384,256]{0,1:T(8,128)(2,1)S(1)}, u32[]{:S(2)}, u32[]{:S(2)}) %collective-permute-start.4) | collective-permute-done | bytes 196640 | tf_op jit(solution)/shard_map/ppermute | solution.py:31
  87.7 0.6 convolution_convert_fusion
  88.7 28.4 %all_to_all.10 = bf16[64,48,128]{2,1,0:T(8,128)(2,1)S(1)} all-to-all(bf16[64,48,128]{2,1,0:T(8,128)(2,1)S(1)} %reshape.72), channel_id=1, replica_groups=mesh['dp'=12,'expert'=64] {'expert'}, dimensions={0} | all-to-all | bytes 1572864 | tf_op jit(solution)/shard_map/all_to_all | solution.py:101
  117.7 27.7 %all-gather = bf16[384,1024]{1,0:T(8,128)(2,1)S(1)} all-gather(bf16[32,1024]{1,0:T(8,128)(2,1)S(1)} %fusion.11), channel_id=2, replica_groups=mesh['dp'=12,'expert'=64] {'dp'}, dimensions={0}, use_global_device_ids=true | all-gather | bytes 851968 | tf_op jit(solution)/shard_map/all_gather | solution.py:164
  145.6 0.7 pad_maximum_fusion.3
  (39 shorter events, 2.5 us)
Async XLA Ops:
  0.0 1.0 copy-start
  5.1 54.0 %all-to-all-start = ((bf16[64,96,128]{2,1,0:T(8,128)(2,1)}), bf16[64,96,128]{2,1,0:T(8,128)(2,1)S(1)}, u32[]{:S(2)}, u32[]{:S(2)}) async-start(bf16[64,96,128]{2,1,0:T(8,128)(2,1)} %bitcast.40), calls=%async_computation | async-start | bytes 3145728 | tf_op jit(solution)/shard_map/all_to_all | solution.py:101
  18.8 1.6 %copy-start.2 = (bf16[1,4096,128]{2,1,0:T(8,128)(2,1)S(1)}, bf16[1,4096,128]{2,1,0:T(8,128)(2,1)}, u32[]{:S(2)}) copy-start(bf16[1,4096,128]{2,1,0:T(8,128)(2,1)} %param.10) | copy-start | bytes 3145732
  19.0 1.7 %copy-start.3 = (bf16[1,4096,128]{2,1,0:T(8,128)(2,1)S(1)}, bf16[1,4096,128]{2,1,0:T(8,128)(2,1)}, u32[]{:S(2)}) copy-start(bf16[1,4096,128]{2,1,0:T(8,128)(2,1)} %param.9) | copy-start | bytes 3145732
  21.0 23.7 %collective-permute-start = (bf16[2560,256]{1,0:T(8,128)(2,1)S(1)}, bf16[2560,256]{1,0:T(8,128)(2,1)S(1)}, u32[]{:S(2)}, u32[]{:S(2)}) collective-permute-start(bf16[2560,256]{1,0:T(8,128)(2,1)S(1)} %slice_dynamic-update-slice_fusion), channel_id=1, source_target_pairs={{0,64},{1,705},{2,66},{3,707},{4,68},{5,709},{6,70},{7,711},{8,72}... | collective-permute-start | bytes 3932168 | tf_op jit(solution)/shard_map/ppermute | solution.py:31
  22.9 35.1 %collective-permute-start.2 = (bf16[128,1024]{1,0:T(8,128)(2,1)S(1)}, bf16[128,1024]{1,0:T(8,128)(2,1)S(1)}, u32[]{:S(2)}, u32[]{:S(2)}) collective-permute-start(bf16[128,1024]{1,0:T(8,128)(2,1)S(1)} %get-tuple-element.27), channel_id=1, source_target_pairs={{0,128},{1,641},{2,130},{3,643},{4,132},{5,645},{6,134},{7,647},{8... | collective-permute-start | bytes 786440 | tf_op jit(solution)/shard_map/ppermute | solution.py:31
  28.4 29.7 %collective-permute-start.1 = (bf16[128,1024]{1,0:T(8,128)(2,1)S(1)}, bf16[128,1024]{1,0:T(8,128)(2,1)S(1)}, u32[]{:S(2)}, u32[]{:S(2)}) collective-permute-start(bf16[128,1024]{1,0:T(8,128)(2,1)S(1)} %get-tuple-element.28), channel_id=1, source_target_pairs={{0,704},{1,65},{2,706},{3,67},{4,708},{5,69},{6,710},{7,71},{8,712... | collective-permute-start | bytes 786440 | tf_op jit(solution)/shard_map/ppermute | solution.py:31
  59.9 2.1 %copy-start.1 = (bf16[2048,256]{1,0:T(8,128)(2,1)S(1)}, bf16[2048,256]{1,0:T(8,128)(2,1)}, u32[]{:S(2)}) copy-start(bf16[2048,256]{1,0:T(8,128)(2,1)} %pad_maximum_fusion) | copy-start | bytes 3145732
  62.0 2.8 %copy-start.5 = (s32[32,8]{0,1:T(8,128)S(1)}, s32[32,8]{0,1:T(8,128)}, u32[]{:S(2)}) copy-start(s32[32,8]{0,1:T(8,128)} %param.7) | copy-start | bytes 3076
  62.0 2.8 %copy-start.6 = (s32[32,8]{0,1:T(8,128)S(1)}, s32[32,8]{0,1:T(8,128)}, u32[]{:S(2)}) copy-start(s32[32,8]{0,1:T(8,128)} %param.8) | copy-start | bytes 3076
  62.8 9.7 %collective-permute-start.3 = (bf16[384,512]{0,1:T(8,128)(2,1)S(1)}, bf16[384,512]{0,1:T(8,128)(2,1)S(1)}, u32[]{:S(2)}, u32[]{:S(2)}) collective-permute-start(bf16[384,512]{0,1:T(8,128)(2,1)S(1)} %pad_maximum_fusion.2), channel_id=1, source_target_pairs={{0,64},{1,705},{2,66},{3,707},{4,68},{5,709},{6,70},{7,711},{8,72}... | collective-permute-start | bytes 1179656 | tf_op jit(solution)/shard_map/ppermute | solution.py:31
  72.5 15.3 %copy-start.4 = (bf16[512,1024]{1,0:T(8,128)(2,1)S(1)}, bf16[512,1024]{1,0:T(8,128)(2,1)}, u32[]{:S(2)}) copy-start(bf16[512,1024]{1,0:T(8,128)(2,1)} %pad_maximum_fusion.1) | copy-start | bytes 3145732
  72.7 15.0 %collective-permute-start.4 = (bf16[384,256]{0,1:T(8,128)(2,1)S(1)}, bf16[384,256]{0,1:T(8,128)(2,1)S(1)}, u32[]{:S(2)}, u32[]{:S(2)}) collective-permute-start(bf16[384,256]{0,1:T(8,128)(2,1)S(1)} %pad_maximum_fusion.4), channel_id=1, source_target_pairs={{0,704},{1,65},{2,706},{3,67},{4,708},{5,69},{6,710},{7,71},{8,712... | collective-permute-start | bytes 589832 | tf_op jit(solution)/shard_map/ppermute | solution.py:31

commit v4 on v3

v4 whole, which is shorter than its diff:
```python
import functools

import jax
import jax.numpy as jnp
from jax import lax
from jax.experimental import pallas as pl
from jax.experimental.pallas import tpu as pltpu
from jax.sharding import PartitionSpec as P

BF16 = jnp.bfloat16
F32 = jnp.float32


def near_of(p, core, n_dp):
    return ((p - core) % n_dp ^ 1) + core


def far_of(p, core, n_dp):
    return near_of(p, 1 - core, n_dp)


def pairs_of(n_dp, n_expert, target):
    pairs = []
    for p in range(n_dp):
        for e in range(n_expert):
            pairs.append((p * n_expert + e, target(p, e % 2) % n_dp * n_expert + e))
    return pairs


def exchange(x, pairs):
    return lax.ppermute(x, ("dp", "expert"), pairs)


def gate_up_kernel(steps, x_ref, gate_ref, up_ref, got_ref, out_ref, acc):
    step = pl.program_id(0)
    ff = out_ref.shape[1] // 2

    @pl.when(step == 0)
    def _():
        acc[...] = jnp.zeros_like(acc)

    own = jnp.concatenate([gate_ref[...], up_ref[...]], axis=1)
    for i, w in enumerate((own, got_ref[...])):
        acc[i] += jnp.dot(x_ref[...], w, preferred_element_type=F32)

    @pl.when(step == steps - 1)
    def _():
        for i in range(2):
            gate, up = acc[i, :, :ff], acc[i, :, ff:]
            act = gate * (1.0 / (1.0 + jnp.exp(-gate))) * up
            out_ref[:, i * ff : (i + 1) * ff] = act.astype(out_ref.dtype)


def gate_up(x, gate, up, got):
    rows, depth = x.shape
    wide = got.shape[1]
    steps = 4
    block = depth // steps
    own = pl.BlockSpec((block, wide // 2), lambda i: (i, 0))
    return pl.pallas_call(
        functools.partial(gate_up_kernel, steps),
        grid=(steps,),
        out_shape=jax.ShapeDtypeStruct((rows, wide), BF16),
        in_specs=[
            pl.BlockSpec((rows, block), lambda i: (0, i)),
            own,
            own,
            pl.BlockSpec((block, wide), lambda i: (i, 0)),
        ],
        out_specs=pl.BlockSpec((rows, wide), lambda i: (0, 0)),
        scratch_shapes=[pltpu.VMEM((2, rows, wide), F32)],
        cost_estimate=pl.CostEstimate(
            flops=4 * rows * depth * wide,
            bytes_accessed=2 * depth * (rows + 2 * wide),
            transcendentals=rows * wide,
        ),
        compiler_params=pltpu.CompilerParams(
            dimension_semantics=("arbitrary",), vmem_limit_bytes=12 << 20
        ),
        name="gate_up",
    )(x, gate, up, got)


def on_device(tokens, expert_ids, gate_ints, w_gate, w_up, w_down):
    n_dp, groups = lax.axis_size("dp"), lax.axis_size("expert")
    tok_rows, feature = tokens.shape
    top = expert_ids.shape[1]
    cap = min(tok_rows, max(2, 3 * tok_rows * top // (2 * groups)))
    rows = groups * cap
    share, quarter = cap // 2, feature // 4
    ff = w_gate.shape[2]
    p = lax.axis_index("dp")
    core = lax.axis_index("expert") % 2

    def near_plane(q):
        return (jnp.mod(q - core, n_dp) ^ 1) + core

    def far_plane(q):
        return (jnp.mod(q - 1 + core, n_dp) ^ 1) + 1 - core

    near = pairs_of(n_dp, groups, lambda q, c: near_of(q, c, n_dp))
    far = pairs_of(n_dp, groups, lambda q, c: far_of(q, c, n_dp))
    cross = pairs_of(
        n_dp, groups, lambda q, c: far_of(near_of(q, c, n_dp) % n_dp, c, n_dp)
    )

    side = p % 2
    row = jnp.arange(groups * share, dtype=jnp.int32)[:, None]
    member = jnp.any(expert_ids.T[:, None, :] == (row // share)[None, :, :], axis=0)
    above = jnp.arange(tok_rows)[:, None] < jnp.arange(tok_rows)[None, :]
    slot = jnp.dot(member.astype(BF16), above.astype(BF16), preferred_element_type=F32)
    wanted = (row % share + side * share).astype(F32)
    place = (member & (slot == wanted)).astype(BF16)
    outgoing = jnp.dot(place, tokens, preferred_element_type=F32).astype(BF16)

    def all_to_all(chunk):
        return lax.all_to_all(chunk, "expert", 0, 0, tiled=True)

    arrived = all_to_all(outgoing.reshape(groups, share * feature // 128, 128))
    arrived = arrived.reshape(groups * share, feature)

    wd = w_down[0]

    def down_for(q):
        return lax.dynamic_slice(wd, (0, jnp.mod(q, 4) * quarter), (ff, quarter))

    q_near, q_far = near_plane(p), far_plane(p)
    q_cross = far_plane(jnp.mod(q_near, n_dp))
    got_gu = exchange(jnp.concatenate([w_gate[0], w_up[0]], axis=1), near)
    got_near = exchange(down_for(q_near), near)
    got_far = exchange(down_for(q_far), far)
    got_cross = exchange(down_for(q_cross), cross)
    down = jnp.concatenate([down_for(p), got_near, got_far, got_cross], axis=0)
    down, late_ids, late_ints = lax.optimization_barrier((down, expert_ids, gate_ints))

    row = jnp.arange(rows, dtype=jnp.int32)[:, None]
    named = late_ids.T[:, None, :] == (row // cap)[None, :, :]
    member = jnp.any(named, axis=0)
    weight = jnp.sum(jnp.where(named, late_ints.T[:, None, :], 0), axis=0)
    slot = jnp.dot(member.astype(BF16), above.astype(BF16), preferred_element_type=F32)
    weight = jnp.where(member & (slot == (row % cap).astype(F32)), weight, 0)
    low = weight % 16
    mixing = jnp.concatenate([(weight - low).astype(BF16), low.astype(BF16)], axis=1)
    arrived, got_gu, down, mixing = lax.optimization_barrier(
        (arrived, got_gu, down, mixing)
    )

    mine = gate_up(arrived, w_gate[0], w_up[0], got_gu)
    other = exchange(mine, near)
    other = jnp.concatenate([other[:, ff:], other[:, :ff]], axis=1)
    hidden = jnp.concatenate(
        [jnp.where(side == 0, mine, other), jnp.where(side == 0, other, mine)], axis=0
    )
    hidden = jnp.concatenate([hidden, exchange(hidden, far)], axis=1)
    partial = jnp.dot(hidden, down, preferred_element_type=F32).astype(BF16)

    chunk = partial.reshape(2, groups, share * quarter // 128, 128)
    chunk = jnp.concatenate([chunk[0], chunk[1]], axis=1)
    back = all_to_all(chunk).reshape(rows, quarter)
    both = lax.dot_general(
        mixing, back, (((0,), (0,)), ((), ())), preferred_element_type=F32
    )
    local = (both[:tok_rows] + both[tok_rows:]) * (1.0 / 1024.0)
    tiles = lax.all_gather(local.astype(BF16), "dp")
    tiles = tiles.reshape(n_dp // 4, 4, tok_rows, quarter).astype(F32).sum(axis=0)
    mixed = jnp.concatenate([tiles[i] for i in range(4)], axis=1)
    return mixed.astype(BF16)


def solution(mesh):
    return jax.shard_map(
        on_device,
        mesh=mesh,
        in_specs=(
            P("expert", None),
            P("expert", None),
            P("expert", None),
            P("expert", None, "dp"),
            P("expert", None, "dp"),
            P("expert", "dp", None),
        ),
        out_specs=P("expert", None),
        check_vma=False,
    )
```

time: 147 us -> 155 us (1.054)
  waiting for transfers between devices: 29.2 us -> 34.3 us
  blocking collectives: 56.1 us -> 60.9 us
  starting transfers between devices: 43.4 us -> 40.4 us
    ppermute x5 -> x6, waiting for transfers between devices: 29.2 us -> 34.3 us  [exchange(): return lax.ppermute(x, ('dp', 'expert'), pairs)]
    all_to_all x1, blocking collectives: 28.4 us -> 33.2 us  [all_to_all(): return lax.all_to_all(chunk, 'expert', 0, 0, tiled=True)]
    ppermute x5 -> x6, starting transfers between devices: 29.8 us -> 25.9 us  [exchange(): return lax.ppermute(x, ('dp', 'expert'), pairs)]
    reshape x3, local copies, waits for them, and re-layouts: 1.38 us -> 4.98 us  [the longest x1 2.55 us: on_device(): arrived = arrived.reshape(groups * share, feature)]
    dot_general x2 -> x1, matrix products: 2.82 us -> 0.79 us  [on_device(): outgoing = jnp.dot(place, tokens, preferred_element_type=F32).astype(BF16)]
  transfers between devices with their start and end apart: 6 -> 7, of which waited for: 4 -> 3; matrix products, arithmetic and copies ran while one was open for 4% -> 4% of each run, Pallas kernels for 0% -> 0%
where the time goes in v4:
time: 155 us; the launch traced here: 154 us
  blocking collectives  60.9 us (39%)
  starting transfers between devices  40.4 us (26%)
  waiting for transfers between devices  34.3 us (22%)
  local copies, waits for them, and re-layouts  6.86 us (4%)
  other arithmetic  4.79 us (3%)
  Pallas kernels  3.46 us (2%)
  matrix products  3.07 us (2%)
    ppermute x6, waiting for transfers between devices, exchange(): return lax.ppermute(x, ('dp', 'expert'), pairs)  34.3 us
    all_to_all x1, blocking collectives, all_to_all(): return lax.all_to_all(chunk, 'expert', 0, 0, tiled=True)  33.2 us
    all_gather x1, blocking collectives, on_device(): tiles = lax.all_gather(local.astype(BF16), 'dp')  27.7 us
    ppermute x6, starting transfers between devices, exchange(): return lax.ppermute(x, ('dp', 'expert'), pairs)  25.9 us
    all_to_all x1, starting transfers between devices, all_to_all(): return lax.all_to_all(chunk, 'expert', 0, 0, tiled=True)  14.5 us
    pallas_call x1, Pallas kernels, gate_up(): pl.pallas_call(functools.partial(gate_up_kernel, steps), grid=(steps,), o...  3.46 us
  transfers between devices with their start and end apart: 7, of which 3 were waited for; matrix products, arithmetic and copies ran while one was open for 4% of the time, Pallas kernels for 0%

profile of v4, /device:TPU:2, one launch (start us, length us, event | category | flops | bytes accessed | tf_op | source)
XLA Modules:
  0.0 154.3 jit_solution(3691347685455887937)
XLA Ops:
  0.0 0.8 compare_reduce_fusion.1
  1.0 0.8 convolution_convert_fusion
  1.8 2.1 %reshape.108 = bf16[64,96,128]{2,1,0:T(8,128)(2,1)} reshape(bf16[192,4096]{1,0:T(8,128)(2,1)S(1)} %convolution_convert_fusion) | data formatting | bytes 3145728 | tf_op jit(solution)/shard_map/reshape | solution.py:119
  3.9 14.5 %all-to-all-start = ((bf16[64,96,128]{2,1,0:T(8,128)(2,1)}), bf16[64,96,128]{2,1,0:T(8,128)(2,1)}, u32[]{:S(2)}, u32[]{:S(2)}) async-start(bf16[64,96,128]{2,1,0:T(8,128)(2,1)} %reshape.108), calls=%async_computation | async-start | bytes 3145728 | tf_op jit(solution)/shard_map/all_to_all | solution.py:117
  18.4 1.6 %pad_maximum_fusion = bf16[4096,256]{1,0:T(8,128)(2,1)} fusion(bf16[4096,128]{1,0:T(8,128)(2,1)S(1)} %bitcast.30, bf16[4096,128]{1,0:T(8,128)(2,1)S(1)} %bitcast.28), kind=kLoop, calls=%fused_computation.1 | loop fusion | flops 4194304 | bytes 4194304 | tf_op jit(solution)/shard_map/concatenate | solution.py:129
  20.0 1.9 %collective-permute-start = (bf16[4096,256]{1,0:T(8,128)(2,1)}, bf16[4096,256]{1,0:T(8,128)(2,1)}, u32[]{:S(2)}, u32[]{:S(2)}) collective-permute-start(bf16[4096,256]{1,0:T(8,128)(2,1)} %pad_maximum_fusion), channel_id=1, source_target_pairs={{0,64},{1,705},{2,66},{3,707},{4,68},{5,709},{6,70},{7,711},{8,72}... | collective-permute-start | bytes 6291464 | tf_op jit(solution)/shard_map/ppermute | solution.py:31
  22.2 4.9 %collective-permute-start.3 = (bf16[128,1024]{1,0:T(8,128)(2,1)S(1)}, bf16[128,1024]{1,0:T(8,128)(2,1)S(1)}, u32[]{:S(2)}, u32[]{:S(2)}) collective-permute-start(bf16[128,1024]{1,0:T(8,128)(2,1)S(1)} %get-tuple-element.21), channel_id=1, source_target_pairs={{0,128},{1,641},{2,130},{3,643},{4,132},{5,645},{6,134},{7,647},{8... | collective-permute-start | bytes 786440 | tf_op jit(solution)/shard_map/ppermute | solution.py:31
  27.1 9.1 %collective-permute-start.2 = (bf16[128,1024]{1,0:T(8,128)(2,1)S(1)}, bf16[128,1024]{1,0:T(8,128)(2,1)S(1)}, u32[]{:S(2)}, u32[]{:S(2)}) collective-permute-start(bf16[128,1024]{1,0:T(8,128)(2,1)S(1)} %get-tuple-element.22), channel_id=1, source_target_pairs={{0,704},{1,65},{2,706},{3,67},{4,708},{5,69},{6,710},{7,71},{8,712... | collective-permute-start | bytes 786440 | tf_op jit(solution)/shard_map/ppermute | solution.py:31
  36.2 2.8 %collective-permute-start.1 = (bf16[128,1024]{1,0:T(8,128)(2,1)S(1)}, bf16[128,1024]{1,0:T(8,128)(2,1)S(1)}, u32[]{:S(2)}, u32[]{:S(2)}) collective-permute-start(bf16[128,1024]{1,0:T(8,128)(2,1)S(1)} %get-tuple-element.20), channel_id=1, source_target_pairs={{0,64},{1,705},{2,66},{3,707},{4,68},{5,709},{6,70},{7,711},{8,72}... | collective-permute-start | bytes 786440 | tf_op jit(solution)/shard_map/ppermute | solution.py:31
  39.1 26.1 %collective-permute-done.3 = bf16[128,1024]{1,0:T(8,128)(2,1)S(1)} collective-permute-done((bf16[128,1024]{1,0:T(8,128)(2,1)S(1)}, bf16[128,1024]{1,0:T(8,128)(2,1)S(1)}, u32[]{:S(2)}, u32[]{:S(2)}) %collective-permute-start.3) | collective-permute-done | bytes 262176 | tf_op jit(solution)/shard_map/ppermute | solution.py:31
  65.2 1.1 pad_maximum_fusion.1
  66.8 2.5 %reshape.109.x_ref = bf16[192,4096]{1,0:T(8,128)(2,1)S(1)} reshape(bf16[64,96,128]{2,1,0:T(8,128)(2,1)} %all-to-all-done) | data formatting | bytes 3145728 | tf_op jit(solution)/shard_map/reshape | solution.py:120
  69.4 1.2 copy-done.3
  70.6 3.5 %gate_up.1 = bf16[192,256]{1,0:T(8,128)(2,1)S(1)} custom-call(bf16[192,4096]{1,0:T(8,128)(2,1)S(1)} %reshape.109.x_ref, bf16[4096,128]{1,0:T(8,128)(2,1)S(1)} %bitcast.29, bf16[4096,128]{1,0:T(8,128)(2,1)S(1)} %bitcast.31, bf16[4096,256]{1,0:T(8,128)(2,1)} %collective-permute-done.got_ref), custom_call_target="tpu_custom_call" | custom-call | flops 805306368 | bytes 5767168 | tf_op jit(solution)/shard_map/gate_up/pallas_call | solution.py:60
  74.1 1.9 %collective-permute-start.4 = (bf16[192,256]{1,0:T(8,128)(2,1)S(1)}, bf16[192,256]{1,0:T(8,128)(2,1)S(1)}, u32[]{:S(2)}, u32[]{:S(2)}) collective-permute-start(bf16[192,256]{1,0:T(8,128)(2,1)S(1)} %gate_up.1), channel_id=1, source_target_pairs={{0,64},{1,705},{2,66},{3,707},{4,68},{5,709},{6,70},{7,711},{8,72}... | collective-permute-start | bytes 294920 | tf_op jit(solution)/shard_map/ppermute | solution.py:31
  76.0 4.6 %collective-permute-done.4 = bf16[192,256]{1,0:T(8,128)(2,1)S(1)} collective-permute-done((bf16[192,256]{1,0:T(8,128)(2,1)S(1)}, bf16[192,256]{1,0:T(8,128)(2,1)S(1)}, u32[]{:S(2)}, u32[]{:S(2)}) %collective-permute-start.4) | collective-permute-done | bytes 98336 | tf_op jit(solution)/shard_map/ppermute | solution.py:31
  80.7 5.2 %collective-permute-start.5 = (bf16[384,256]{1,0:T(8,128)(2,1)S(1)}, bf16[384,256]{1,0:T(8,128)(2,1)S(1)}, u32[]{:S(2)}, u32[]{:S(2)}) collective-permute-start(bf16[384,256]{1,0:T(8,128)(2,1)S(1)} %pad_maximum_fusion.4), channel_id=1, source_target_pairs={{0,704},{1,65},{2,706},{3,67},{4,708},{5,69},{6,710},{7,71},{8,712... | collective-permute-start | bytes 589832 | tf_op jit(solution)/shard_map/ppermute | solution.py:31
  85.9 3.6 %collective-permute-done.5 = bf16[384,256]{1,0:T(8,128)(2,1)S(1)} collective-permute-done((bf16[384,256]{1,0:T(8,128)(2,1)S(1)}, bf16[384,256]{1,0:T(8,128)(2,1)S(1)}, u32[]{:S(2)}, u32[]{:S(2)}) %collective-permute-start.5) | collective-permute-done | bytes 196640 | tf_op jit(solution)/shard_map/ppermute | solution.py:31
  89.5 1.8 %convolution_convert_fusion.1 = bf16[384,1024]{1,0:T(8,128)(2,1)S(1)} fusion(bf16[512,1024]{1,0:T(8,128)(2,1)} %pad_maximum_fusion.1, bf16[384,256]{1,0:T(8,128)(2,1)S(1)} %collective-permute-done.5, bf16[192,256]{1,0:T(8,128)(2,1)S(1)} %get-tuple-element.30, bf16[192,256]{1,0:T(8,128)(2,1)S(1)} %get-tuple-element.29), kind=kOutput, calls=%fused_computation.2 | convolution fusion | flops 404226048 | bytes 2228224 | tf_op jit(solution)/shard_map/dot_general | solution.py:155
  91.9 33.2 %all_to_all.10 = bf16[64,48,128]{2,1,0:T(8,128)(2,1)S(1)} all-to-all(bf16[64,48,128]{2,1,0:T(8,128)(2,1)S(1)} %pad_maximum_fusion.2), channel_id=1, replica_groups=mesh['dp'=12,'expert'=64] {'expert'}, dimensions={0} | all-to-all | bytes 1572864 | tf_op jit(solution)/shard_map/all_to_all | solution.py:117
  125.1 0.3 reshape.110
  125.4 0.3 fusion.29
  125.7 27.7 %all-gather = bf16[384,1024]{1,0:T(8,128)(2,1)S(1)} all-gather(bf16[32,1024]{1,0:T(8,128)(2,1)S(1)} %fusion.10), channel_id=2, replica_groups=mesh['dp'=12,'expert'=64] {'dp'}, dimensions={0}, use_global_device_ids=true | all-gather | bytes 851968 | tf_op jit(solution)/shard_map/all_gather | solution.py:164
  153.6 0.7 pad_maximum_fusion.3
  (35 shorter events, 1.5 us)
Async XLA Ops:
  0.0 1.0 copy-start
  3.9 14.5 %copy-start.1 = (bf16[1,4096,128]{2,1,0:T(8,128)(2,1)S(1)}, bf16[1,4096,128]{2,1,0:T(8,128)(2,1)}, u32[]{:S(2)}) copy-start(bf16[1,4096,128]{2,1,0:T(8,128)(2,1)} %param.9) | copy-start | bytes 3145732
  3.9 14.6 %copy-start.2 = (bf16[1,4096,128]{2,1,0:T(8,128)(2,1)S(1)}, bf16[1,4096,128]{2,1,0:T(8,128)(2,1)}, u32[]{:S(2)}) copy-start(bf16[1,4096,128]{2,1,0:T(8,128)(2,1)} %param.10) | copy-start | bytes 3145732
  3.9 62.9 %all-to-all-start = ((bf16[64,96,128]{2,1,0:T(8,128)(2,1)}), bf16[64,96,128]{2,1,0:T(8,128)(2,1)}, u32[]{:S(2)}, u32[]{:S(2)}) async-start(bf16[64,96,128]{2,1,0:T(8,128)(2,1)} %reshape.108), calls=%async_computation | async-start | bytes 3145728 | tf_op jit(solution)/shard_map/all_to_all | solution.py:117
  18.4 3.6 %copy-start.4 = (bf16[1,128,4096]{2,1,0:T(8,128)(2,1)S(1)}, bf16[1,128,4096]{2,1,0:T(8,128)(2,1)}, u32[]{:S(2)}) copy-start(bf16[1,128,4096]{2,1,0:T(8,128)(2,1)} %param.11) | copy-start | bytes 3145732
  20.0 49.4 %collective-permute-start = (bf16[4096,256]{1,0:T(8,128)(2,1)}, bf16[4096,256]{1,0:T(8,128)(2,1)}, u32[]{:S(2)}, u32[]{:S(2)}) collective-permute-start(bf16[4096,256]{1,0:T(8,128)(2,1)} %pad_maximum_fusion), channel_id=1, source_target_pairs={{0,64},{1,705},{2,66},{3,707},{4,68},{5,709},{6,70},{7,711},{8,72}... | collective-permute-start | bytes 6291464 | tf_op jit(solution)/shard_map/ppermute | solution.py:31
  22.1 44.2 %copy-start.5 = (s32[32,8]{0,1:T(8,128)S(1)}, s32[32,8]{0,1:T(8,128)}, u32[]{:S(2)}) copy-start(s32[32,8]{0,1:T(8,128)} %param.7) | copy-start | bytes 3076
  22.1 44.3 %copy-start.6 = (s32[32,8]{0,1:T(8,128)S(1)}, s32[32,8]{0,1:T(8,128)}, u32[]{:S(2)}) copy-start(s32[32,8]{0,1:T(8,128)} %param.8) | copy-start | bytes 3076
  22.2 43.0 %collective-permute-start.3 = (bf16[128,1024]{1,0:T(8,128)(2,1)S(1)}, bf16[128,1024]{1,0:T(8,128)(2,1)S(1)}, u32[]{:S(2)}, u32[]{:S(2)}) collective-permute-start(bf16[128,1024]{1,0:T(8,128)(2,1)S(1)} %get-tuple-element.21), channel_id=1, source_target_pairs={{0,128},{1,641},{2,130},{3,643},{4,132},{5,645},{6,134},{7,647},{8... | collective-permute-start | bytes 786440 | tf_op jit(solution)/shard_map/ppermute | solution.py:31
  27.1 38.1 %collective-permute-start.2 = (bf16[128,1024]{1,0:T(8,128)(2,1)S(1)}, bf16[128,1024]{1,0:T(8,128)(2,1)S(1)}, u32[]{:S(2)}, u32[]{:S(2)}) collective-permute-start(bf16[128,1024]{1,0:T(8,128)(2,1)S(1)} %get-tuple-element.22), channel_id=1, source_target_pairs={{0,704},{1,65},{2,706},{3,67},{4,708},{5,69},{6,710},{7,71},{8,712... | collective-permute-start | bytes 786440 | tf_op jit(solution)/shard_map/ppermute | solution.py:31
  36.2 29.0 %collective-permute-start.1 = (bf16[128,1024]{1,0:T(8,128)(2,1)S(1)}, bf16[128,1024]{1,0:T(8,128)(2,1)S(1)}, u32[]{:S(2)}, u32[]{:S(2)}) collective-permute-start(bf16[128,1024]{1,0:T(8,128)(2,1)S(1)} %get-tuple-element.20), channel_id=1, source_target_pairs={{0,64},{1,705},{2,66},{3,707},{4,68},{5,709},{6,70},{7,711},{8,72}... | collective-permute-start | bytes 786440 | tf_op jit(solution)/shard_map/ppermute | solution.py:31
  69.4 1.2 copy-start.3
  74.1 6.5 %collective-permute-start.4 = (bf16[192,256]{1,0:T(8,128)(2,1)S(1)}, bf16[192,256]{1,0:T(8,128)(2,1)S(1)}, u32[]{:S(2)}, u32[]{:S(2)}) collective-permute-start(bf16[192,256]{1,0:T(8,128)(2,1)S(1)} %gate_up.1), channel_id=1, source_target_pairs={{0,64},{1,705},{2,66},{3,707},{4,68},{5,709},{6,70},{7,711},{8,72}... | collective-permute-start | bytes 294920 | tf_op jit(solution)/shard_map/ppermute | solution.py:31
  80.7 8.9 %collective-permute-start.5 = (bf16[384,256]{1,0:T(8,128)(2,1)S(1)}, bf16[384,256]{1,0:T(8,128)(2,1)S(1)}, u32[]{:S(2)}, u32[]{:S(2)}) collective-permute-start(bf16[384,256]{1,0:T(8,128)(2,1)S(1)} %pad_maximum_fusion.4), channel_id=1, source_target_pairs={{0,704},{1,65},{2,706},{3,67},{4,708},{5,69},{6,710},{7,71},{8,712... | collective-permute-start | bytes 589832 | tf_op jit(solution)/shard_map/ppermute | solution.py:31

commit v5 on v3

--- a/solution.py
+++ b/solution.py
@@ -1,10 +1,6 @@
-import functools
-
 import jax
 import jax.numpy as jnp
 from jax import lax
-from jax.experimental import pallas as pl
-from jax.experimental.pallas import tpu as pltpu
 from jax.sharding import PartitionSpec as P
 
 BF16 = jnp.bfloat16
@@ -31,43 +27,6 @@
     return lax.ppermute(x, ("dp", "expert"), pairs)
 
 
-def place_rows(cap, ids_ref, tok_ref, out_ref, used):
-    top, tok_rows = ids_ref.shape
-
-    def clear(i, carry):
-        out_ref[i] = jnp.zeros(out_ref.shape[1:], out_ref.dtype)
-        return carry
-
-    lax.fori_loop(0, out_ref.shape[0], clear, 0, unroll=16)
-    for e in range(used.shape[0]):
-        used[e] = 0
-
-    def one(t, carry):
-        row = tok_ref[t]
-        experts = [ids_ref[k, t] for k in range(top)]
-        slots = [used[e] for e in experts]
-        for e, slot in zip(experts, slots):
-            out_ref[e * cap + slot] = row
-            used[e] = slot + 1
-        return carry
-
-    lax.fori_loop(0, tok_rows, one, 0, unroll=4)
-
-
-def dispatch_rows(ids, tok, groups, cap):
-    return pl.pallas_call(
-        functools.partial(place_rows, cap),
-        out_shape=jax.ShapeDtypeStruct((groups * cap,) + tok.shape[1:], tok.dtype),
-        in_specs=[
-            pl.BlockSpec(memory_space=pltpu.SMEM),
-            pl.BlockSpec(memory_space=pltpu.VMEM),
-        ],
-        out_specs=pl.BlockSpec(memory_space=pltpu.VMEM),
-        scratch_shapes=[pltpu.SMEM((groups,), jnp.int32)],
-        name="place_rows",
-    )(ids, tok)
-
-
 def on_device(tokens, expert_ids, gate_ints, w_gate, w_up, w_down):
     n_dp, groups = lax.axis_size("dp"), lax.axis_size("expert")
     tok_rows, feature = tokens.shape
@@ -91,10 +50,20 @@
         n_dp, groups, lambda q, c: far_of(near_of(q, c, n_dp) % n_dp, c, n_dp)
     )
 
+    row = jnp.arange(rows, dtype=jnp.int32)[:, None]
+    above = jnp.arange(tok_rows)[:, None] < jnp.arange(tok_rows)[None, :]
+
+    def placement(ids):
+        named = ids.T[:, None, :] == (row // cap)[None, :, :]
+        member = jnp.any(named, axis=0)
+        slot = jnp.dot(
+            member.astype(BF16), above.astype(BF16), preferred_element_type=F32
+        )
+        return named, member & (slot == (row % cap).astype(F32))
+
+    place = placement(expert_ids)[1].astype(BF16)
     tok_half = lax.dynamic_slice(tokens, (0, p % 2 * half), (tok_rows, half))
-    outgoing = dispatch_rows(
-        expert_ids.T, tok_half.reshape(tok_rows, half // 128, 128), groups, cap
-    )
+    outgoing = jnp.dot(place, tok_half, preferred_element_type=F32).astype(BF16)
 
     def all_to_all(chunk, width):
         chunk = chunk.reshape(groups, cap * width // 128, 128)
@@ -135,13 +104,9 @@
     theirs = jnp.dot(arrived, got_gu, preferred_element_type=F32)
     other = exchange(jnp.concatenate([mine, theirs], axis=1).astype(BF16), near)
 
-    row = jnp.arange(rows, dtype=jnp.int32)[:, None]
-    named = late_ids.T[:, None, :] == (row // cap)[None, :, :]
-    member = jnp.any(named, axis=0)
+    named, placed = placement(late_ids)
     weight = jnp.sum(jnp.where(named, late_ints.T[:, None, :], 0), axis=0)
-    above = jnp.arange(tok_rows)[:, None] < jnp.arange(tok_rows)[None, :]
-    slot = jnp.dot(member.astype(BF16), above.astype(BF16), preferred_element_type=F32)
-    weight = jnp.where(member & (slot == (row % cap).astype(F32)), weight, 0)
+    weight = jnp.where(placed, weight, 0)
     low = weight % 16
     mixing = jnp.concatenate([(weight - low).astype(BF16), low.astype(BF16)], axis=1)
     other, mixing = lax.optimization_barrier((other, mixing))

time: 147 us -> 146 us (level)
  Pallas kernels: 3.49 us -> 0 us
    pallas_call x1 -> x0, Pallas kernels: 3.49 us -> none  [dispatch_rows(): pl.pallas_call(functools.partial(place_rows, cap), out_shape=jax.ShapeDty...]
    reshape x1 -> x2, local copies, waits for them, and re-layouts: 0.33 us -> 2.46 us  [all_to_all(): chunk = chunk.reshape(groups, cap * width // 128, 128)]
  transfers between devices with their start and end apart: 6 -> 6, of which waited for: 4 -> 4; matrix products, arithmetic and copies ran while one was open for 4% -> 3% of each run, Pallas kernels for 0% -> 0%
where the time goes in v5:
time: 146 us; the launch traced here: 145 us
  blocking collectives  56.1 us (38%)
  starting transfers between devices  43.4 us (30%)
  waiting for transfers between devices  29.2 us (20%)
  local copies, waits for them, and re-layouts  6.59 us (5%)
  matrix products  4.7 us (3%)
  other arithmetic  4.57 us (3%)
    ppermute x5, starting transfers between devices, exchange(): return lax.ppermute(x, ('dp', 'expert'), pairs)  29.8 us
    ppermute x5, waiting for transfers between devices, exchange(): return lax.ppermute(x, ('dp', 'expert'), pairs)  29.2 us
    all_to_all x1, blocking collectives, all_to_all(): chunk = lax.all_to_all(chunk, 'expert', 0, 0, tiled=True)  28.4 us
    all_gather x1, blocking collectives, on_device(): tiles = lax.all_gather(local.astype(BF16), 'dp')  27.7 us
    all_to_all x1, starting transfers between devices, all_to_all(): chunk = lax.all_to_all(chunk, 'expert', 0, 0, tiled=True)  13.6 us
  transfers between devices with their start and end apart: 6, of which 4 were waited for; matrix products, arithmetic and copies ran while one was open for 3% of the time, Pallas kernels for 0%

profile of v5, /device:TPU:2, one launch (start us, length us, event | category | flops | bytes accessed | tf_op | source)
XLA Modules:
  0.0 145.1 jit_solution(18058816603303240553)
XLA Ops:
  0.0 0.8 compare_reduce_fusion.1
  1.0 0.8 convolution_convert_fusion
  1.8 2.1 %reshape.67 = bf16[64,96,128]{2,1,0:T(8,128)(2,1)} reshape(bf16[384,2048]{1,0:T(8,128)(2,1)S(1)} %convolution_convert_fusion) | data formatting | bytes 3145728 | tf_op jit(solution)/shard_map/reshape | solution.py:69
  3.9 13.6 %all-to-all-start = ((bf16[64,96,128]{2,1,0:T(8,128)(2,1)}), bf16[64,96,128]{2,1,0:T(8,128)(2,1)S(1)}, u32[]{:S(2)}, u32[]{:S(2)}) async-start(bf16[64,96,128]{2,1,0:T(8,128)(2,1)} %reshape.67), calls=%async_computation | async-start | bytes 3145728 | tf_op jit(solution)/shard_map/all_to_all | solution.py:70
  17.8 1.4 dynamic-slice_bitcast_fusion.6
  19.8 1.9 %collective-permute-start = (bf16[2560,256]{1,0:T(8,128)(2,1)S(1)}, bf16[2560,256]{1,0:T(8,128)(2,1)S(1)}, u32[]{:S(2)}, u32[]{:S(2)}) collective-permute-start(bf16[2560,256]{1,0:T(8,128)(2,1)S(1)} %slice_dynamic-update-slice_fusion), channel_id=1, source_target_pairs={{0,64},{1,705},{2,66},{3,707},{4,68},{5,709},{6,70},{7,711},{8,72}... | collective-permute-start | bytes 3932168 | tf_op jit(solution)/shard_map/ppermute | solution.py:27
  21.7 5.5 %collective-permute-start.2 = (bf16[128,1024]{1,0:T(8,128)(2,1)S(1)}, bf16[128,1024]{1,0:T(8,128)(2,1)S(1)}, u32[]{:S(2)}, u32[]{:S(2)}) collective-permute-start(bf16[128,1024]{1,0:T(8,128)(2,1)S(1)} %get-tuple-element.27), channel_id=1, source_target_pairs={{0,128},{1,641},{2,130},{3,643},{4,132},{5,645},{6,134},{7,647},{8... | collective-permute-start | bytes 786440 | tf_op jit(solution)/shard_map/ppermute | solution.py:27
  27.2 9.1 %collective-permute-start.1 = (bf16[128,1024]{1,0:T(8,128)(2,1)S(1)}, bf16[128,1024]{1,0:T(8,128)(2,1)S(1)}, u32[]{:S(2)}, u32[]{:S(2)}) collective-permute-start(bf16[128,1024]{1,0:T(8,128)(2,1)S(1)} %get-tuple-element.28), channel_id=1, source_target_pairs={{0,704},{1,65},{2,706},{3,67},{4,708},{5,69},{6,710},{7,71},{8,712... | collective-permute-start | bytes 786440 | tf_op jit(solution)/shard_map/ppermute | solution.py:27
  36.3 1.1 pad_maximum_fusion
  37.4 6.1 %collective-permute-done = bf16[2560,256]{1,0:T(8,128)(2,1)S(1)} collective-permute-done((bf16[2560,256]{1,0:T(8,128)(2,1)S(1)}, bf16[2560,256]{1,0:T(8,128)(2,1)S(1)}, u32[]{:S(2)}, u32[]{:S(2)}) %collective-permute-start) | collective-permute-done | bytes 1310752 | tf_op jit(solution)/shard_map/ppermute | solution.py:27
  43.5 1.1 copy-done.1
  44.6 12.3 %collective-permute-done.2 = bf16[128,1024]{1,0:T(8,128)(2,1)S(1)} collective-permute-done((bf16[128,1024]{1,0:T(8,128)(2,1)S(1)}, bf16[128,1024]{1,0:T(8,128)(2,1)S(1)}, u32[]{:S(2)}, u32[]{:S(2)}) %collective-permute-start.2) | collective-permute-done | bytes 262176 | tf_op jit(solution)/shard_map/ppermute | solution.py:27
  56.9 1.1 pad_maximum_fusion.1
  57.9 0.7 reshape.68
  58.7 2.1 %fusion.29 = (bf16[384,256]{0,1:T(8,128)(2,1)S(1)}, f32[384,256]{0,1:T(8,128)S(1)}) fusion(bf16[384,2048]{1,0:T(8,128)(2,1)S(1)} %reshape.68, bf16[2048,256]{1,0:T(8,128)(2,1)} %pad_maximum_fusion), kind=kOutput, calls=%fused_computation.73 | convolution fusion | flops 402751488 | bytes 3211264 | tf_op jit(solution)/shard_map/dot_general | solution.py:103
  60.8 0.8 fusion.28
  61.6 1.9 %collective-permute-start.3 = (bf16[384,512]{0,1:T(8,128)(2,1)S(1)}, bf16[384,512]{0,1:T(8,128)(2,1)S(1)}, u32[]{:S(2)}, u32[]{:S(2)}) collective-permute-start(bf16[384,512]{0,1:T(8,128)(2,1)S(1)} %pad_maximum_fusion.2), channel_id=1, source_target_pairs={{0,64},{1,705},{2,66},{3,707},{4,68},{5,709},{6,70},{7,711},{8,72}... | collective-permute-start | bytes 1179656 | tf_op jit(solution)/shard_map/ppermute | solution.py:27
  64.1 7.2 %collective-permute-done.3 = bf16[384,512]{0,1:T(8,128)(2,1)S(1)} collective-permute-done((bf16[384,512]{0,1:T(8,128)(2,1)S(1)}, bf16[384,512]{0,1:T(8,128)(2,1)S(1)}, u32[]{:S(2)}, u32[]{:S(2)}) %collective-permute-start.3) | collective-permute-done | bytes 393248 | tf_op jit(solution)/shard_map/ppermute | solution.py:27
  71.5 11.3 %collective-permute-start.4 = (bf16[384,256]{0,1:T(8,128)(2,1)S(1)}, bf16[384,256]{0,1:T(8,128)(2,1)S(1)}, u32[]{:S(2)}, u32[]{:S(2)}) collective-permute-start(bf16[384,256]{0,1:T(8,128)(2,1)S(1)} %pad_maximum_fusion.4), channel_id=1, source_target_pairs={{0,704},{1,65},{2,706},{3,67},{4,708},{5,69},{6,710},{7,71},{8,712... | collective-permute-start | bytes 589832 | tf_op jit(solution)/shard_map/ppermute | solution.py:27
  82.9 3.6 %collective-permute-done.4 = bf16[384,256]{0,1:T(8,128)(2,1)S(1)} collective-permute-done((bf16[384,256]{0,1:T(8,128)(2,1)S(1)}, bf16[384,256]{0,1:T(8,128)(2,1)S(1)}, u32[]{:S(2)}, u32[]{:S(2)}) %collective-permute-start.4) | collective-permute-done | bytes 196640 | tf_op jit(solution)/shard_map/ppermute | solution.py:27
  86.5 0.6 convolution_convert_fusion.1
  87.5 28.4 %all_to_all.10 = bf16[64,48,128]{2,1,0:T(8,128)(2,1)S(1)} all-to-all(bf16[64,48,128]{2,1,0:T(8,128)(2,1)S(1)} %reshape.69), channel_id=1, replica_groups=mesh['dp'=12,'expert'=64] {'expert'}, dimensions={0} | all-to-all | bytes 1572864 | tf_op jit(solution)/shard_map/all_to_all | solution.py:70
  116.5 27.7 %all-gather = bf16[384,1024]{1,0:T(8,128)(2,1)S(1)} all-gather(bf16[32,1024]{1,0:T(8,128)(2,1)S(1)} %fusion.12), channel_id=2, replica_groups=mesh['dp'=12,'expert'=64] {'dp'}, dimensions={0}, use_global_device_ids=true | all-gather | bytes 851968 | tf_op jit(solution)/shard_map/all_gather | solution.py:129
  144.4 0.7 pad_maximum_fusion.3
  (40 shorter events, 2.6 us)
Async XLA Ops:
  0.0 1.0 copy-start
  3.9 54.0 %all-to-all-start = ((bf16[64,96,128]{2,1,0:T(8,128)(2,1)}), bf16[64,96,128]{2,1,0:T(8,128)(2,1)S(1)}, u32[]{:S(2)}, u32[]{:S(2)}) async-start(bf16[64,96,128]{2,1,0:T(8,128)(2,1)} %reshape.67), calls=%async_computation | async-start | bytes 3145728 | tf_op jit(solution)/shard_map/all_to_all | solution.py:70
  17.5 1.6 %copy-start.2 = (bf16[1,4096,128]{2,1,0:T(8,128)(2,1)S(1)}, bf16[1,4096,128]{2,1,0:T(8,128)(2,1)}, u32[]{:S(2)}) copy-start(bf16[1,4096,128]{2,1,0:T(8,128)(2,1)} %param.10) | copy-start | bytes 3145732
  17.8 1.7 %copy-start.3 = (bf16[1,4096,128]{2,1,0:T(8,128)(2,1)S(1)}, bf16[1,4096,128]{2,1,0:T(8,128)(2,1)}, u32[]{:S(2)}) copy-start(bf16[1,4096,128]{2,1,0:T(8,128)(2,1)} %param.9) | copy-start | bytes 3145732
  19.8 23.7 %collective-permute-start = (bf16[2560,256]{1,0:T(8,128)(2,1)S(1)}, bf16[2560,256]{1,0:T(8,128)(2,1)S(1)}, u32[]{:S(2)}, u32[]{:S(2)}) collective-permute-start(bf16[2560,256]{1,0:T(8,128)(2,1)S(1)} %slice_dynamic-update-slice_fusion), channel_id=1, source_target_pairs={{0,64},{1,705},{2,66},{3,707},{4,68},{5,709},{6,70},{7,711},{8,72}... | collective-permute-start | bytes 3932168 | tf_op jit(solution)/shard_map/ppermute | solution.py:27
  21.7 35.1 %collective-permute-start.2 = (bf16[128,1024]{1,0:T(8,128)(2,1)S(1)}, bf16[128,1024]{1,0:T(8,128)(2,1)S(1)}, u32[]{:S(2)}, u32[]{:S(2)}) collective-permute-start(bf16[128,1024]{1,0:T(8,128)(2,1)S(1)} %get-tuple-element.27), channel_id=1, source_target_pairs={{0,128},{1,641},{2,130},{3,643},{4,132},{5,645},{6,134},{7,647},{8... | collective-permute-start | bytes 786440 | tf_op jit(solution)/shard_map/ppermute | solution.py:27
  27.2 29.7 %collective-permute-start.1 = (bf16[128,1024]{1,0:T(8,128)(2,1)S(1)}, bf16[128,1024]{1,0:T(8,128)(2,1)S(1)}, u32[]{:S(2)}, u32[]{:S(2)}) collective-permute-start(bf16[128,1024]{1,0:T(8,128)(2,1)S(1)} %get-tuple-element.28), channel_id=1, source_target_pairs={{0,704},{1,65},{2,706},{3,67},{4,708},{5,69},{6,710},{7,71},{8,712... | collective-permute-start | bytes 786440 | tf_op jit(solution)/shard_map/ppermute | solution.py:27
  43.5 1.1 copy-start.1
  58.7 2.1 %slice-start = ((bf16[2560,256]{1,0:T(8,128)(2,1)}), bf16[2048,256]{1,0:T(8,128)(2,1)S(1)}, s32[]{:S(2)}) async-start(bf16[2560,256]{1,0:T(8,128)(2,1)} %copy-done.1), calls=%async_computation.2 | async-start | bytes 2097152 | tf_op jit(solution)/shard_map/slice | solution.py:100
  60.8 2.8 %copy-start.5 = (s32[32,8]{0,1:T(8,128)S(1)}, s32[32,8]{0,1:T(8,128)}, u32[]{:S(2)}) copy-start(s32[32,8]{0,1:T(8,128)} %param.7) | copy-start | bytes 3076
  60.8 2.8 %copy-start.6 = (s32[32,8]{0,1:T(8,128)S(1)}, s32[32,8]{0,1:T(8,128)}, u32[]{:S(2)}) copy-start(s32[32,8]{0,1:T(8,128)} %param.8) | copy-start | bytes 3076
  61.6 9.7 %collective-permute-start.3 = (bf16[384,512]{0,1:T(8,128)(2,1)S(1)}, bf16[384,512]{0,1:T(8,128)(2,1)S(1)}, u32[]{:S(2)}, u32[]{:S(2)}) collective-permute-start(bf16[384,512]{0,1:T(8,128)(2,1)S(1)} %pad_maximum_fusion.2), channel_id=1, source_target_pairs={{0,64},{1,705},{2,66},{3,707},{4,68},{5,709},{6,70},{7,711},{8,72}... | collective-permute-start | bytes 1179656 | tf_op jit(solution)/shard_map/ppermute | solution.py:27
  71.3 15.3 %copy-start.4 = (bf16[512,1024]{1,0:T(8,128)(2,1)S(1)}, bf16[512,1024]{1,0:T(8,128)(2,1)}, u32[]{:S(2)}) copy-start(bf16[512,1024]{1,0:T(8,128)(2,1)} %pad_maximum_fusion.1) | copy-start | bytes 3145732
  71.5 15.0 %collective-permute-start.4 = (bf16[384,256]{0,1:T(8,128)(2,1)S(1)}, bf16[384,256]{0,1:T(8,128)(2,1)S(1)}, u32[]{:S(2)}, u32[]{:S(2)}) collective-permute-start(bf16[384,256]{0,1:T(8,128)(2,1)S(1)} %pad_maximum_fusion.4), channel_id=1, source_target_pairs={{0,704},{1,65},{2,706},{3,67},{4,708},{5,69},{6,710},{7,71},{8,712... | collective-permute-start | bytes 589832 | tf_op jit(solution)/shard_map/ppermute | solution.py:27

commit v6 on v5

--- a/solution.py
+++ b/solution.py
@@ -83,26 +83,21 @@
             [lax.dynamic_slice(w, at, (half, ff)) for w in (wg, wu)], axis=1
         )
 
-    folds = quarter // (2 * ff)
     q_near, q_far = jnp.mod(near_plane(p), n_dp), jnp.mod(far_plane(p), n_dp)
     q_cross = jnp.mod(far_plane(q_near), n_dp)
-    for_near = down_for(q_near)
-    folded = [for_near[:, i * 2 * ff : (i + 1) * 2 * ff] for i in range(folds)]
-    got = exchange(jnp.concatenate([gate_up_for(q_near)] + folded, axis=0), near)
+    got_gu = exchange(gate_up_for(q_near), near)
+    got_near = exchange(down_for(q_near), near)
     got_far = exchange(down_for(q_far), far)
     got_cross = exchange(down_for(q_cross), cross)
-    got_near = jnp.concatenate(
-        [got[half + i * ff : half + (i + 1) * ff] for i in range(folds)], axis=1
-    )
     down = jnp.concatenate([down_for(p), got_near, got_far, got_cross], axis=0)
-    own_gu = gate_up_for(p)
-    arrived, own_gu, got_gu, down, late_ids, late_ints = lax.optimization_barrier(
-        (arrived, own_gu, got[:half], down, expert_ids, gate_ints)
+    weights = jnp.concatenate([gate_up_for(p), got_gu], axis=1)
+    arrived, weights, down, late_ids, late_ints = lax.optimization_barrier(
+        (arrived, weights, down, expert_ids, gate_ints)
     )
 
-    mine = jnp.dot(arrived, own_gu, preferred_element_type=F32)
-    theirs = jnp.dot(arrived, got_gu, preferred_element_type=F32)
-    other = exchange(jnp.concatenate([mine, theirs], axis=1).astype(BF16), near)
+    parts = jnp.dot(arrived, weights, preferred_element_type=F32)
+    other = exchange(parts.astype(BF16), near)
+    mine, theirs = parts[:, : 2 * ff], parts[:, 2 * ff :]
 
     named, placed = placement(late_ids)
     weight = jnp.sum(jnp.where(named, late_ints.T[:, None, :], 0), axis=0)

time: 146 us -> 145 us (level)
  waiting for transfers between devices: 29.2 us -> 24.6 us
  other arithmetic: 4.57 us -> 7.13 us
  starting transfers between devices: 43.4 us -> 45.4 us
    ppermute x5 -> x6, waiting for transfers between devices: 29.2 us -> 24.6 us  [exchange(): return lax.ppermute(x, ('dp', 'expert'), pairs)]
    concatenate x1, other arithmetic: 0.04 us -> 2.75 us  [on_device(): weights = jnp.concatenate([gate_up_for(p), got_gu], axis=1)]
    ppermute x5 -> x6, starting transfers between devices: 29.8 us -> 31.8 us  [exchange(): return lax.ppermute(x, ('dp', 'expert'), pairs)]
    dynamic_slice x1, local copies, waits for them, and re-layouts: 0.14 us -> 1.66 us  [gate_up_for(): lax.dynamic_slice(w, at, (half, ff))]
  transfers between devices with their start and end apart: 6 -> 7, of which waited for: 4 -> 3; matrix products, arithmetic and copies ran while one was open for 3% -> 6% of each run, Pallas kernels for 0% -> 0%
where the time goes in v6:
time: 145 us
  blocking collectives  56.1 us (39%)
  starting transfers between devices  45.4 us (31%)
  waiting for transfers between devices  24.6 us (17%)
  other arithmetic  7.13 us (5%)
  local copies, waits for them, and re-layouts  6.52 us (4%)
  matrix products  4.43 us (3%)
    ppermute x6, starting transfers between devices, exchange(): return lax.ppermute(x, ('dp', 'expert'), pairs)  31.8 us
    all_to_all x1, blocking collectives, all_to_all(): chunk = lax.all_to_all(chunk, 'expert', 0, 0, tiled=True)  28.4 us
    all_gather x1, blocking collectives, on_device(): tiles = lax.all_gather(local.astype(BF16), 'dp')  27.7 us
    ppermute x6, waiting for transfers between devices, exchange(): return lax.ppermute(x, ('dp', 'expert'), pairs)  24.6 us
    all_to_all x1, starting transfers between devices, all_to_all(): chunk = lax.all_to_all(chunk, 'expert', 0, 0, tiled=True)  13.6 us
  transfers between devices with their start and end apart: 7, of which 3 were waited for; matrix products, arithmetic and copies ran while one was open for 6% of the time, Pallas kernels for 0%

profile of v6, /device:TPU:2, one launch (start us, length us, event | category | flops | bytes accessed | tf_op | source)
XLA Modules:
  0.0 144.7 jit_solution(14505831901013476076)
XLA Ops:
  0.0 0.8 compare_reduce_fusion.1
  1.0 0.8 convolution_convert_fusion
  1.8 2.1 %reshape.67 = bf16[64,96,128]{2,1,0:T(8,128)(2,1)} reshape(bf16[384,2048]{1,0:T(8,128)(2,1)S(1)} %convolution_convert_fusion) | data formatting | bytes 3145728 | tf_op jit(solution)/shard_map/reshape | solution.py:69
  3.9 13.6 %all-to-all-start = ((bf16[64,96,128]{2,1,0:T(8,128)(2,1)}), bf16[64,96,128]{2,1,0:T(8,128)(2,1)S(1)}, u32[]{:S(2)}, u32[]{:S(2)}) async-start(bf16[64,96,128]{2,1,0:T(8,128)(2,1)} %reshape.67), calls=%async_computation | async-start | bytes 3145728 | tf_op jit(solution)/shard_map/all_to_all | solution.py:70
  17.6 1.7 %dynamic-slice_bitcast_fusion.2 = (bf16[2048,128]{1,0:T(8,128)(2,1)S(1)}, bf16[2048,128]{1,0:T(8,128)(2,1)S(1)}, bf16[2048,128]{1,0:T(8,128)(2,1)S(1)}, bf16[2048,128]{1,0:T(8,128)(2,1)S(1)}) fusion(bf16[1,4096,128]{2,1,0:T(8,128)(2,1)} %param.10, s32[]{:T(128)S(6)} %select_n.124, s32[]{:T(128)S(6)} %select_n.129, bf16[1,4096,128]{2,1,0:T(8,128)(2,1)} %param.9), kind=kLoop, calls=%fused_computation.12 | loop fusion | bytes 4194312 | tf_op jit(solution)/shard_map/dynamic_slice | solution.py:83
  19.2 1.1 pad_maximum_fusion.1
  20.3 1.9 %collective-permute-start = (bf16[2048,256]{1,0:T(8,128)(2,1)}, bf16[2048,256]{1,0:T(8,128)(2,1)}, u32[]{:S(2)}, u32[]{:S(2)}) collective-permute-start(bf16[2048,256]{1,0:T(8,128)(2,1)} %pad_maximum_fusion.1), channel_id=1, source_target_pairs={{0,64},{1,705},{2,66},{3,707},{4,68},{5,709},{6,70},{7,711},{8,72}... | collective-permute-start | bytes 3145736 | tf_op jit(solution)/shard_map/ppermute | solution.py:27
  22.4 1.3 dynamic-slice_bitcast_fusion.7
  23.7 5.5 %collective-permute-start.3 = (bf16[128,1024]{1,0:T(8,128)(2,1)S(1)}, bf16[128,1024]{1,0:T(8,128)(2,1)S(1)}, u32[]{:S(2)}, u32[]{:S(2)}) collective-permute-start(bf16[128,1024]{1,0:T(8,128)(2,1)S(1)} %get-tuple-element.23), channel_id=1, source_target_pairs={{0,128},{1,641},{2,130},{3,643},{4,132},{5,645},{6,134},{7,647},{8... | collective-permute-start | bytes 786440 | tf_op jit(solution)/shard_map/ppermute | solution.py:27
  29.1 9.1 %collective-permute-start.2 = (bf16[128,1024]{1,0:T(8,128)(2,1)S(1)}, bf16[128,1024]{1,0:T(8,128)(2,1)S(1)}, u32[]{:S(2)}, u32[]{:S(2)}) collective-permute-start(bf16[128,1024]{1,0:T(8,128)(2,1)S(1)} %get-tuple-element.24), channel_id=1, source_target_pairs={{0,704},{1,65},{2,706},{3,67},{4,708},{5,69},{6,710},{7,71},{8,712... | collective-permute-start | bytes 786440 | tf_op jit(solution)/shard_map/ppermute | solution.py:27
  38.3 2.8 %collective-permute-start.1 = (bf16[128,1024]{1,0:T(8,128)(2,1)S(1)}, bf16[128,1024]{1,0:T(8,128)(2,1)S(1)}, u32[]{:S(2)}, u32[]{:S(2)}) collective-permute-start(bf16[128,1024]{1,0:T(8,128)(2,1)S(1)} %get-tuple-element.22), channel_id=1, source_target_pairs={{0,64},{1,705},{2,66},{3,707},{4,68},{5,709},{6,70},{7,711},{8,72}... | collective-permute-start | bytes 786440 | tf_op jit(solution)/shard_map/ppermute | solution.py:27
  41.1 13.7 %collective-permute-done.3 = bf16[128,1024]{1,0:T(8,128)(2,1)S(1)} collective-permute-done((bf16[128,1024]{1,0:T(8,128)(2,1)S(1)}, bf16[128,1024]{1,0:T(8,128)(2,1)S(1)}, u32[]{:S(2)}, u32[]{:S(2)}) %collective-permute-start.3) | collective-permute-done | bytes 262176 | tf_op jit(solution)/shard_map/ppermute | solution.py:27
  54.9 1.1 pad_maximum_fusion.2
  56.0 2.8 %pad_maximum_fusion = bf16[2048,512]{1,0:T(8,128)(2,1)} fusion(bf16[2048,256]{1,0:T(8,128)(2,1)} %collective-permute-done, bf16[2048,128]{1,0:T(8,128)(2,1)S(1)} %get-tuple-element.27, bf16[2048,128]{1,0:T(8,128)(2,1)S(1)} %get-tuple-element.40), kind=kLoop, calls=%fused_computation.1 | loop fusion | flops 6291456 | bytes 4194304 | tf_op jit(solution)/shard_map/concatenate | solution.py:93
  58.7 0.7 reshape.68
  59.5 2.6 %fusion.27 = (bf16[384,512]{1,0:T(8,128)(2,1)S(1)}, f32[384,512]{1,0:T(8,128)S(1)}) fusion(bf16[384,2048]{1,0:T(8,128)(2,1)S(1)} %reshape.68, bf16[2048,512]{1,0:T(8,128)(2,1)} %pad_maximum_fusion), kind=kOutput, calls=%fused_computation.66 | convolution fusion | flops 805502976 | bytes 4849664 | tf_op jit(solution)/shard_map/dot_general | solution.py:98
  62.0 2.1 %collective-permute-start.4 = (bf16[384,512]{1,0:T(8,128)(2,1)S(1)}, bf16[384,512]{1,0:T(8,128)(2,1)S(1)}, u32[]{:S(2)}, u32[]{:S(2)}) collective-permute-start(bf16[384,512]{1,0:T(8,128)(2,1)S(1)} %get-tuple-element.35), channel_id=1, source_target_pairs={{0,64},{1,705},{2,66},{3,707},{4,68},{5,709},{6,70},{7,711},{8,72}... | collective-permute-start | bytes 1179656 | tf_op jit(solution)/shard_map/ppermute | solution.py:27
  64.6 7.2 %collective-permute-done.4 = bf16[384,512]{1,0:T(8,128)(2,1)S(1)} collective-permute-done((bf16[384,512]{1,0:T(8,128)(2,1)S(1)}, bf16[384,512]{1,0:T(8,128)(2,1)S(1)}, u32[]{:S(2)}, u32[]{:S(2)}) %collective-permute-start.4) | collective-permute-done | bytes 393248 | tf_op jit(solution)/shard_map/ppermute | solution.py:27
  72.1 10.4 %collective-permute-start.5 = (bf16[384,256]{1,0:T(8,128)(2,1)S(1)}, bf16[384,256]{1,0:T(8,128)(2,1)S(1)}, u32[]{:S(2)}, u32[]{:S(2)}) collective-permute-start(bf16[384,256]{1,0:T(8,128)(2,1)S(1)} %pad_maximum_fusion.4), channel_id=1, source_target_pairs={{0,704},{1,65},{2,706},{3,67},{4,708},{5,69},{6,710},{7,71},{8,712... | collective-permute-start | bytes 589832 | tf_op jit(solution)/shard_map/ppermute | solution.py:27
  82.5 3.6 %collective-permute-done.5 = bf16[384,256]{1,0:T(8,128)(2,1)S(1)} collective-permute-done((bf16[384,256]{1,0:T(8,128)(2,1)S(1)}, bf16[384,256]{1,0:T(8,128)(2,1)S(1)}, u32[]{:S(2)}, u32[]{:S(2)}) %collective-permute-start.5) | collective-permute-done | bytes 196640 | tf_op jit(solution)/shard_map/ppermute | solution.py:27
  86.2 0.6 convolution_convert_fusion.1
  87.1 28.4 %all_to_all.10 = bf16[64,48,128]{2,1,0:T(8,128)(2,1)S(1)} all-to-all(bf16[64,48,128]{2,1,0:T(8,128)(2,1)S(1)} %reshape.69), channel_id=1, replica_groups=mesh['dp'=12,'expert'=64] {'expert'}, dimensions={0} | all-to-all | bytes 1572864 | tf_op jit(solution)/shard_map/all_to_all | solution.py:70
  116.1 27.7 %all-gather = bf16[384,1024]{1,0:T(8,128)(2,1)S(1)} all-gather(bf16[32,1024]{1,0:T(8,128)(2,1)S(1)} %fusion.12), channel_id=2, replica_groups=mesh['dp'=12,'expert'=64] {'dp'}, dimensions={0}, use_global_device_ids=true | all-gather | bytes 851968 | tf_op jit(solution)/shard_map/all_gather | solution.py:124
  144.0 0.7 pad_maximum_fusion.3
  (27 shorter events, 1.9 us)
Async XLA Ops:
  0.0 1.0 copy-start
  3.9 54.8 %all-to-all-start = ((bf16[64,96,128]{2,1,0:T(8,128)(2,1)}), bf16[64,96,128]{2,1,0:T(8,128)(2,1)S(1)}, u32[]{:S(2)}, u32[]{:S(2)}) async-start(bf16[64,96,128]{2,1,0:T(8,128)(2,1)} %reshape.67), calls=%async_computation | async-start | bytes 3145728 | tf_op jit(solution)/shard_map/all_to_all | solution.py:70
  20.3 35.6 %collective-permute-start = (bf16[2048,256]{1,0:T(8,128)(2,1)}, bf16[2048,256]{1,0:T(8,128)(2,1)}, u32[]{:S(2)}, u32[]{:S(2)}) collective-permute-start(bf16[2048,256]{1,0:T(8,128)(2,1)} %pad_maximum_fusion.1), channel_id=1, source_target_pairs={{0,64},{1,705},{2,66},{3,707},{4,68},{5,709},{6,70},{7,711},{8,72}... | collective-permute-start | bytes 3145736 | tf_op jit(solution)/shard_map/ppermute | solution.py:27
  23.7 31.2 %collective-permute-start.3 = (bf16[128,1024]{1,0:T(8,128)(2,1)S(1)}, bf16[128,1024]{1,0:T(8,128)(2,1)S(1)}, u32[]{:S(2)}, u32[]{:S(2)}) collective-permute-start(bf16[128,1024]{1,0:T(8,128)(2,1)S(1)} %get-tuple-element.23), channel_id=1, source_target_pairs={{0,128},{1,641},{2,130},{3,643},{4,132},{5,645},{6,134},{7,647},{8... | collective-permute-start | bytes 786440 | tf_op jit(solution)/shard_map/ppermute | solution.py:27
  29.1 25.7 %collective-permute-start.2 = (bf16[128,1024]{1,0:T(8,128)(2,1)S(1)}, bf16[128,1024]{1,0:T(8,128)(2,1)S(1)}, u32[]{:S(2)}, u32[]{:S(2)}) collective-permute-start(bf16[128,1024]{1,0:T(8,128)(2,1)S(1)} %get-tuple-element.24), channel_id=1, source_target_pairs={{0,704},{1,65},{2,706},{3,67},{4,708},{5,69},{6,710},{7,71},{8,712... | collective-permute-start | bytes 786440 | tf_op jit(solution)/shard_map/ppermute | solution.py:27
  38.3 16.6 %collective-permute-start.1 = (bf16[128,1024]{1,0:T(8,128)(2,1)S(1)}, bf16[128,1024]{1,0:T(8,128)(2,1)S(1)}, u32[]{:S(2)}, u32[]{:S(2)}) collective-permute-start(bf16[128,1024]{1,0:T(8,128)(2,1)S(1)} %get-tuple-element.22), channel_id=1, source_target_pairs={{0,64},{1,705},{2,66},{3,707},{4,68},{5,709},{6,70},{7,711},{8,72}... | collective-permute-start | bytes 786440 | tf_op jit(solution)/shard_map/ppermute | solution.py:27
  59.4 4.7 %copy-start.2 = (s32[32,8]{0,1:T(8,128)S(1)}, s32[32,8]{0,1:T(8,128)}, u32[]{:S(2)}) copy-start(s32[32,8]{0,1:T(8,128)} %param.7) | copy-start | bytes 3076
  59.4 4.7 %copy-start.3 = (s32[32,8]{0,1:T(8,128)S(1)}, s32[32,8]{0,1:T(8,128)}, u32[]{:S(2)}) copy-start(s32[32,8]{0,1:T(8,128)} %param.8) | copy-start | bytes 3076
  62.0 24.1 %copy-start.1 = (bf16[512,1024]{1,0:T(8,128)(2,1)S(1)}, bf16[512,1024]{1,0:T(8,128)(2,1)}, u32[]{:S(2)}) copy-start(bf16[512,1024]{1,0:T(8,128)(2,1)} %pad_maximum_fusion.2) | copy-start | bytes 3145732
  62.0 9.8 %collective-permute-start.4 = (bf16[384,512]{1,0:T(8,128)(2,1)S(1)}, bf16[384,512]{1,0:T(8,128)(2,1)S(1)}, u32[]{:S(2)}, u32[]{:S(2)}) collective-permute-start(bf16[384,512]{1,0:T(8,128)(2,1)S(1)} %get-tuple-element.35), channel_id=1, source_target_pairs={{0,64},{1,705},{2,66},{3,707},{4,68},{5,709},{6,70},{7,711},{8,72}... | collective-permute-start | bytes 1179656 | tf_op jit(solution)/shard_map/ppermute | solution.py:27
  72.1 14.0 %collective-permute-start.5 = (bf16[384,256]{1,0:T(8,128)(2,1)S(1)}, bf16[384,256]{1,0:T(8,128)(2,1)S(1)}, u32[]{:S(2)}, u32[]{:S(2)}) collective-permute-start(bf16[384,256]{1,0:T(8,128)(2,1)S(1)} %pad_maximum_fusion.4), channel_id=1, source_target_pairs={{0,704},{1,65},{2,706},{3,67},{4,708},{5,69},{6,710},{7,71},{8,712... | collective-permute-start | bytes 589832 | tf_op jit(solution)/shard_map/ppermute | solution.py:27

commit v7 on v6

--- a/solution.py
+++ b/solution.py
@@ -90,11 +90,12 @@
     got_far = exchange(down_for(q_far), far)
     got_cross = exchange(down_for(q_cross), cross)
     down = jnp.concatenate([down_for(p), got_near, got_far, got_cross], axis=0)
-    weights = jnp.concatenate([gate_up_for(p), got_gu], axis=1)
-    arrived, weights, down, late_ids, late_ints = lax.optimization_barrier(
-        (arrived, weights, down, expert_ids, gate_ints)
+    own_gu = gate_up_for(p)
+    arrived, own_gu, got_gu, down, late_ids, late_ints = lax.optimization_barrier(
+        (arrived, own_gu, got_gu, down, expert_ids, gate_ints)
     )
 
+    weights = jnp.concatenate([own_gu, got_gu], axis=1)
     parts = jnp.dot(arrived, weights, preferred_element_type=F32)
     other = exchange(parts.astype(BF16), near)
     mine, theirs = parts[:, : 2 * ff], parts[:, 2 * ff :]

time: 145 us -> 145 us (level)
  other arithmetic: 7.13 us -> 5.5 us
    concatenate x1 -> x0, other arithmetic: 2.75 us -> none  [on_device(): weights = jnp.concatenate([gate_up_for(p), got_gu], axis=1)]
  transfers between devices with their start and end apart: 7 -> 7, of which waited for: 3 -> 3; matrix products, arithmetic and copies ran while one was open for 6% -> 5% of each run, Pallas kernels for 0% -> 0%
where the time goes in v7:
time: 145 us
  blocking collectives  56.1 us (39%)
  starting transfers between devices  46 us (32%)
  waiting for transfers between devices  25.6 us (18%)
  local copies, waits for them, and re-layouts  6.55 us (5%)
  other arithmetic  5.5 us (4%)
  matrix products  4.37 us (3%)
    ppermute x6, starting transfers between devices, exchange(): return lax.ppermute(x, ('dp', 'expert'), pairs)  32.4 us
    all_to_all x1, blocking collectives, all_to_all(): chunk = lax.all_to_all(chunk, 'expert', 0, 0, tiled=True)  28.4 us
    all_gather x1, blocking collectives, on_device(): tiles = lax.all_gather(local.astype(BF16), 'dp')  27.7 us
    ppermute x6, waiting for transfers between devices, exchange(): return lax.ppermute(x, ('dp', 'expert'), pairs)  25.6 us
    all_to_all x1, starting transfers between devices, all_to_all(): chunk = lax.all_to_all(chunk, 'expert', 0, 0, tiled=True)  13.6 us
  transfers between devices with their start and end apart: 7, of which 3 were waited for; matrix products, arithmetic and copies ran while one was open for 5% of the time, Pallas kernels for 0%

profile of v7, /device:TPU:2, one launch (start us, length us, event | category | flops | bytes accessed | tf_op | source)
XLA Modules:
  0.0 144.7 jit_solution(8005191294508200723)
XLA Ops:
  0.0 0.8 compare_reduce_fusion.1
  1.0 0.8 convolution_convert_fusion
  1.8 2.1 %reshape.67 = bf16[64,96,128]{2,1,0:T(8,128)(2,1)} reshape(bf16[384,2048]{1,0:T(8,128)(2,1)S(1)} %convolution_convert_fusion) | data formatting | bytes 3145728 | tf_op jit(solution)/shard_map/reshape | solution.py:69
  3.9 13.6 %all-to-all-start = ((bf16[64,96,128]{2,1,0:T(8,128)(2,1)}), bf16[64,96,128]{2,1,0:T(8,128)(2,1)S(1)}, u32[]{:S(2)}, u32[]{:S(2)}) async-start(bf16[64,96,128]{2,1,0:T(8,128)(2,1)} %reshape.67), calls=%async_computation | async-start | bytes 3145728 | tf_op jit(solution)/shard_map/all_to_all | solution.py:70
  17.6 1.7 %dynamic-slice_bitcast_fusion = (bf16[2048,128]{1,0:T(8,128)(2,1)S(1)}, bf16[2048,128]{1,0:T(8,128)(2,1)S(1)}, bf16[2048,128]{1,0:T(8,128)(2,1)S(1)}, bf16[2048,128]{1,0:T(8,128)(2,1)S(1)}) fusion(bf16[1,4096,128]{2,1,0:T(8,128)(2,1)} %param.10, s32[]{:T(128)S(6)} %select_n.129, s32[]{:T(128)S(6)} %select_n.124, bf16[1,4096,128]{2,1,0:T(8,128)(2,1)} %param.9), kind=kLoop, calls=%fused_computation.14 | loop fusion | bytes 4194312 | tf_op jit(solution)/shard_map/dynamic_slice | solution.py:83
  19.3 1.1 pad_maximum_fusion.1
  20.4 1.9 %collective-permute-start = (bf16[2048,256]{1,0:T(8,128)(2,1)}, bf16[2048,256]{1,0:T(8,128)(2,1)}, u32[]{:S(2)}, u32[]{:S(2)}) collective-permute-start(bf16[2048,256]{1,0:T(8,128)(2,1)} %pad_maximum_fusion.1), channel_id=1, source_target_pairs={{0,64},{1,705},{2,66},{3,707},{4,68},{5,709},{6,70},{7,711},{8,72}... | collective-permute-start | bytes 3145736 | tf_op jit(solution)/shard_map/ppermute | solution.py:27
  22.4 1.3 dynamic-slice_bitcast_fusion.7
  23.7 3.9 %collective-permute-start.1 = (bf16[128,1024]{1,0:T(8,128)(2,1)S(1)}, bf16[128,1024]{1,0:T(8,128)(2,1)S(1)}, u32[]{:S(2)}, u32[]{:S(2)}) collective-permute-start(bf16[128,1024]{1,0:T(8,128)(2,1)S(1)} %get-tuple-element.24), channel_id=1, source_target_pairs={{0,64},{1,705},{2,66},{3,707},{4,68},{5,709},{6,70},{7,711},{8,72}... | collective-permute-start | bytes 786440 | tf_op jit(solution)/shard_map/ppermute | solution.py:27
  27.6 3.5 %collective-permute-start.3 = (bf16[128,1024]{1,0:T(8,128)(2,1)S(1)}, bf16[128,1024]{1,0:T(8,128)(2,1)S(1)}, u32[]{:S(2)}, u32[]{:S(2)}) collective-permute-start(bf16[128,1024]{1,0:T(8,128)(2,1)S(1)} %get-tuple-element.25), channel_id=1, source_target_pairs={{0,128},{1,641},{2,130},{3,643},{4,132},{5,645},{6,134},{7,647},{8... | collective-permute-start | bytes 786440 | tf_op jit(solution)/shard_map/ppermute | solution.py:27
  31.1 10.6 %collective-permute-start.2 = (bf16[128,1024]{1,0:T(8,128)(2,1)S(1)}, bf16[128,1024]{1,0:T(8,128)(2,1)S(1)}, u32[]{:S(2)}, u32[]{:S(2)}) collective-permute-start(bf16[128,1024]{1,0:T(8,128)(2,1)S(1)} %get-tuple-element.26), channel_id=1, source_target_pairs={{0,704},{1,65},{2,706},{3,67},{4,708},{5,69},{6,710},{7,71},{8,712... | collective-permute-start | bytes 786440 | tf_op jit(solution)/shard_map/ppermute | solution.py:27
  41.7 1.1 pad_maximum_fusion
  42.8 14.8 %collective-permute-done.3 = bf16[128,1024]{1,0:T(8,128)(2,1)S(1)} collective-permute-done((bf16[128,1024]{1,0:T(8,128)(2,1)S(1)}, bf16[128,1024]{1,0:T(8,128)(2,1)S(1)}, u32[]{:S(2)}, u32[]{:S(2)}) %collective-permute-start.3) | collective-permute-done | bytes 262176 | tf_op jit(solution)/shard_map/ppermute | solution.py:27
  57.6 1.0 pad_maximum_fusion.2
  58.7 0.7 reshape.68
  59.4 2.5 %fusion.32 = (bf16[384,512]{1,0:T(8,128)(2,1)S(1)}, f32[384,512]{1,0:T(8,128)S(1)}) fusion(bf16[384,2048]{1,0:T(8,128)(2,1)S(1)} %reshape.68, bf16[2048,256]{1,0:T(8,128)(2,1)} %collective-permute-done, bf16[2048,256]{1,0:T(8,128)(2,1)} %pad_maximum_fusion), kind=kOutput, calls=%fused_computation.71 | convolution fusion | flops 809697280 | bytes 4849664 | tf_op jit(solution)/shard_map/dot_general | solution.py:99
  61.9 1.9 %collective-permute-start.4 = (bf16[384,512]{1,0:T(8,128)(2,1)S(1)}, bf16[384,512]{1,0:T(8,128)(2,1)S(1)}, u32[]{:S(2)}, u32[]{:S(2)}) collective-permute-start(bf16[384,512]{1,0:T(8,128)(2,1)S(1)} %get-tuple-element.37), channel_id=1, source_target_pairs={{0,64},{1,705},{2,66},{3,707},{4,68},{5,709},{6,70},{7,711},{8,72}... | collective-permute-start | bytes 1179656 | tf_op jit(solution)/shard_map/ppermute | solution.py:27
  64.4 7.2 %collective-permute-done.4 = bf16[384,512]{1,0:T(8,128)(2,1)S(1)} collective-permute-done((bf16[384,512]{1,0:T(8,128)(2,1)S(1)}, bf16[384,512]{1,0:T(8,128)(2,1)S(1)}, u32[]{:S(2)}, u32[]{:S(2)}) %collective-permute-start.4) | collective-permute-done | bytes 393248 | tf_op jit(solution)/shard_map/ppermute | solution.py:27
  71.9 10.6 %collective-permute-start.5 = (bf16[384,256]{1,0:T(8,128)(2,1)S(1)}, bf16[384,256]{1,0:T(8,128)(2,1)S(1)}, u32[]{:S(2)}, u32[]{:S(2)}) collective-permute-start(bf16[384,256]{1,0:T(8,128)(2,1)S(1)} %pad_maximum_fusion.4), channel_id=1, source_target_pairs={{0,704},{1,65},{2,706},{3,67},{4,708},{5,69},{6,710},{7,71},{8,712... | collective-permute-start | bytes 589832 | tf_op jit(solution)/shard_map/ppermute | solution.py:27
  82.5 3.6 %collective-permute-done.5 = bf16[384,256]{1,0:T(8,128)(2,1)S(1)} collective-permute-done((bf16[384,256]{1,0:T(8,128)(2,1)S(1)}, bf16[384,256]{1,0:T(8,128)(2,1)S(1)}, u32[]{:S(2)}, u32[]{:S(2)}) %collective-permute-start.5) | collective-permute-done | bytes 196640 | tf_op jit(solution)/shard_map/ppermute | solution.py:27
  86.1 0.6 convolution_convert_fusion.1
  87.0 28.4 %all_to_all.10 = bf16[64,48,128]{2,1,0:T(8,128)(2,1)S(1)} all-to-all(bf16[64,48,128]{2,1,0:T(8,128)(2,1)S(1)} %reshape.69), channel_id=1, replica_groups=mesh['dp'=12,'expert'=64] {'expert'}, dimensions={0} | all-to-all | bytes 1572864 | tf_op jit(solution)/shard_map/all_to_all | solution.py:70
  116.0 27.7 %all-gather = bf16[384,1024]{1,0:T(8,128)(2,1)S(1)} all-gather(bf16[32,1024]{1,0:T(8,128)(2,1)S(1)} %fusion.16), channel_id=2, replica_groups=mesh['dp'=12,'expert'=64] {'dp'}, dimensions={0}, use_global_device_ids=true | all-gather | bytes 851968 | tf_op jit(solution)/shard_map/all_gather | solution.py:125
  143.9 0.7 pad_maximum_fusion.3
  (27 shorter events, 1.9 us)
Async XLA Ops:
  0.0 1.0 copy-start
  3.9 54.8 %all-to-all-start = ((bf16[64,96,128]{2,1,0:T(8,128)(2,1)}), bf16[64,96,128]{2,1,0:T(8,128)(2,1)S(1)}, u32[]{:S(2)}, u32[]{:S(2)}) async-start(bf16[64,96,128]{2,1,0:T(8,128)(2,1)} %reshape.67), calls=%async_computation | async-start | bytes 3145728 | tf_op jit(solution)/shard_map/all_to_all | solution.py:70
  20.4 39.1 %collective-permute-start = (bf16[2048,256]{1,0:T(8,128)(2,1)}, bf16[2048,256]{1,0:T(8,128)(2,1)}, u32[]{:S(2)}, u32[]{:S(2)}) collective-permute-start(bf16[2048,256]{1,0:T(8,128)(2,1)} %pad_maximum_fusion.1), channel_id=1, source_target_pairs={{0,64},{1,705},{2,66},{3,707},{4,68},{5,709},{6,70},{7,711},{8,72}... | collective-permute-start | bytes 3145736 | tf_op jit(solution)/shard_map/ppermute | solution.py:27
  23.7 19.1 %collective-permute-start.1 = (bf16[128,1024]{1,0:T(8,128)(2,1)S(1)}, bf16[128,1024]{1,0:T(8,128)(2,1)S(1)}, u32[]{:S(2)}, u32[]{:S(2)}) collective-permute-start(bf16[128,1024]{1,0:T(8,128)(2,1)S(1)} %get-tuple-element.24), channel_id=1, source_target_pairs={{0,64},{1,705},{2,66},{3,707},{4,68},{5,709},{6,70},{7,711},{8,72}... | collective-permute-start | bytes 786440 | tf_op jit(solution)/shard_map/ppermute | solution.py:27
  27.6 30.0 %collective-permute-start.3 = (bf16[128,1024]{1,0:T(8,128)(2,1)S(1)}, bf16[128,1024]{1,0:T(8,128)(2,1)S(1)}, u32[]{:S(2)}, u32[]{:S(2)}) collective-permute-start(bf16[128,1024]{1,0:T(8,128)(2,1)S(1)} %get-tuple-element.25), channel_id=1, source_target_pairs={{0,128},{1,641},{2,130},{3,643},{4,132},{5,645},{6,134},{7,647},{8... | collective-permute-start | bytes 786440 | tf_op jit(solution)/shard_map/ppermute | solution.py:27
  31.1 26.5 %collective-permute-start.2 = (bf16[128,1024]{1,0:T(8,128)(2,1)S(1)}, bf16[128,1024]{1,0:T(8,128)(2,1)S(1)}, u32[]{:S(2)}, u32[]{:S(2)}) collective-permute-start(bf16[128,1024]{1,0:T(8,128)(2,1)S(1)} %get-tuple-element.26), channel_id=1, source_target_pairs={{0,704},{1,65},{2,706},{3,67},{4,708},{5,69},{6,710},{7,71},{8,712... | collective-permute-start | bytes 786440 | tf_op jit(solution)/shard_map/ppermute | solution.py:27
  59.4 4.5 %copy-start.2 = (s32[32,8]{0,1:T(8,128)S(1)}, s32[32,8]{0,1:T(8,128)}, u32[]{:S(2)}) copy-start(s32[32,8]{0,1:T(8,128)} %param.7) | copy-start | bytes 3076
  59.4 4.5 %copy-start.3 = (s32[32,8]{0,1:T(8,128)S(1)}, s32[32,8]{0,1:T(8,128)}, u32[]{:S(2)}) copy-start(s32[32,8]{0,1:T(8,128)} %param.8) | copy-start | bytes 3076
  61.9 9.7 %collective-permute-start.4 = (bf16[384,512]{1,0:T(8,128)(2,1)S(1)}, bf16[384,512]{1,0:T(8,128)(2,1)S(1)}, u32[]{:S(2)}, u32[]{:S(2)}) collective-permute-start(bf16[384,512]{1,0:T(8,128)(2,1)S(1)} %get-tuple-element.37), channel_id=1, source_target_pairs={{0,64},{1,705},{2,66},{3,707},{4,68},{5,709},{6,70},{7,711},{8,72}... | collective-permute-start | bytes 1179656 | tf_op jit(solution)/shard_map/ppermute | solution.py:27
  71.6 14.5 %copy-start.1 = (bf16[512,1024]{1,0:T(8,128)(2,1)S(1)}, bf16[512,1024]{1,0:T(8,128)(2,1)}, u32[]{:S(2)}) copy-start(bf16[512,1024]{1,0:T(8,128)(2,1)} %pad_maximum_fusion.2) | copy-start | bytes 3145732
  71.9 14.2 %collective-permute-start.5 = (bf16[384,256]{1,0:T(8,128)(2,1)S(1)}, bf16[384,256]{1,0:T(8,128)(2,1)S(1)}, u32[]{:S(2)}, u32[]{:S(2)}) collective-permute-start(bf16[384,256]{1,0:T(8,128)(2,1)S(1)} %pad_maximum_fusion.4), channel_id=1, source_target_pairs={{0,704},{1,65},{2,706},{3,67},{4,708},{5,69},{6,710},{7,71},{8,712... | collective-permute-start | bytes 589832 | tf_op jit(solution)/shard_map/ppermute | solution.py:27
